TPU v7x, 32 devices: a whole 2x2x4 slice. The times are simulated.
32 devices in a mesh: groups: 1, expert: 16 (over z, y, x), replica: 2 (over core).
Axes of the slice: x: 2, y: 2, z: 4, core: 2. Of those that a mesh axis runs over, the one named last changes fastest.
Arguments:
- queries: bfloat16 [128, 8192], P(('groups', 'expert', 'replica')), may hold values from -250 to 250
- token_keys: bfloat16 [128, 512], P(('groups', 'expert', 'replica')), may hold values from -6 to 6
- token_values: bfloat16 [128, 512], P(('groups', 'expert', 'replica')), may hold values from -6 to 6
- stored_keys: bfloat16 [128, 256, 512], P(('groups', 'expert', 'replica')), may hold values from -7 to 7
- stored_values: bfloat16 [128, 256, 512], P(('groups', 'expert', 'replica')), may hold values from -6 to 6
- kv_len: int32 [128], P(('groups', 'expert', 'replica')), may hold values from 2 to 256, as said below
- residual: bfloat16 [128, 4096], P(('groups', 'expert', 'replica')), may hold values from -6 to 6
- out_weight: bfloat16 [8192, 4096], P(('expert', 'replica')), may hold values from -0.1875 to 0.1875
- norm_gain: bfloat16 [4096], replicated, may hold values from 0.25 to 1.75
- expert_ids: int32 [128, 8], P(('groups', 'expert')), may hold values from 0 to 15, all different within a row; in each aligned block of 8 rows (0 to 7, 8 to 15, ...) at most 4 rows name the same one
- route_weight: float32 [128, 8], P(('groups', 'expert')), may hold values from 0.05 to 1
- w_gate: bfloat16 [16, 4096, 768], P('expert', None, 'replica'), may hold values from -0.09375 to 0.09375
- w_up: bfloat16 [16, 4096, 768], P('expert', None, 'replica'), may hold values from -0.09375 to 0.09375
- w_down: bfloat16 [16, 768, 4096], P('expert', 'replica'), may hold values from -0.4375 to 0.4375
Outputs:
- updated: bfloat16 [128, 4096], P(('groups', 'expert', 'replica'))
Inputs may be any that keep to these rules, and one draw needn't show every extreme that they name: `kv_len`: at least 2; some sequence uses all 256 positions. `expert_ids`: each token names 8 different experts; in each aligned block of 8 tokens no expert is named by more than 4 tokens, and some block reaches it.
All inputs are finite; a program needn't handle non-finite values.
Results may differ from a plain program's by a relative error of at most 0.01.
Values may be sent and summed in bfloat16 or wider, within the bound.
A program may use at most 64 MiB of HBM per device.

v0:
```python
import functools
import math

import jax
import jax.numpy as jnp
from jax import lax
from jax.experimental import pallas as pl
from jax.experimental.pallas import tpu as pltpu
from jax.sharding import PartitionSpec as P

HEAD_WIDTH = 128
TILE = 16
CHUNKS = 1
MESH = pl.DeviceIdType.MESH
F32 = jnp.float32
BF16 = jnp.bfloat16


def regroup(outer, inner, back=False):
    size = 8 * outer * inner
    shape = (8 * TILE, size) if back else (size, 8 * TILE)
    a = lax.broadcasted_iota(jnp.int32, shape, 1 if back else 0)
    b = lax.broadcasted_iota(jnp.int32, shape, 0 if back else 1)
    o = a // (8 * inner)
    j = (a // inner) % 8
    i = a % inner
    return jnp.where(b == j * TILE + o * inner + i, 1.0, 0.0).astype(BF16)


def dot(a, b):
    return jnp.dot(a, b, preferred_element_type=F32)


def flipped(index, mask, bits):
    total = 0
    for k in range(bits):
        place = 1 << k
        total = total + lax.rem(lax.div(index, place) + lax.div(mask, place), 2) * place
    return total


def kernel(
    E, cap,
    q_hbm, tk_hbm, tv_hbm, kv_hbm, res_hbm, gain_hbm, ids_hbm, rw_hbm,
    k_hbm, v_hbm, ow_hbm, wg_hbm, wu_hbm, wd_hbm,
    out_ref,
    q_ref, tk_ref, tv_ref, kv_ref, res_ref, gain_ref, ids_ref, rw_ref,
    kb, vb, ow, wg, wu, wd,
    qs, tks, tvs, att, ratt, asm, yb, rs, resb, resp, hs, ssb, ssp,
    tts, whi, wlo, xb, xr, xs, hid, os, zb, zr, ub, up_,
    lsem, osem, wsem, isem, psend, precv, s1, r1, s2, r2, s3, r3, s4, r4,
):
    N = 2 * E
    e_me = lax.axis_index("expert")
    c = lax.axis_index("replica")
    rank = e_me * 2 + c
    S = q_ref.shape[0]
    T = 2 * S
    heads = q_ref.shape[1] // HEAD_WIDTH
    G = tk_ref.shape[1] // HEAD_WIDTH
    width = heads // G
    L = k_hbm.shape[1]
    D = res_ref.shape[1]
    half = D // 2
    hpc = heads // E
    Q = TILE // cap
    cw = half // Q
    mine = pl.ds(pl.multiple_of(c * half, half), half)
    other = pl.ds(pl.multiple_of((1 - c) * half, half), half)
    partner = {"expert": e_me, "replica": 1 - c}

    small = [
        pltpu.make_async_copy(src, dst, isem.at[k])
        for k, (src, dst) in enumerate((
            (q_hbm, q_ref), (tk_hbm, tk_ref), (tv_hbm, tv_ref), (kv_hbm, kv_ref),
            (res_hbm, res_ref), (gain_hbm, gain_ref), (ids_hbm, ids_ref), (rw_hbm, rw_ref),
        ))
    ]
    for cp in small:
        cp.start()
    barrier = pltpu.get_barrier_semaphore()

    @pl.loop(1, N)
    def _(i):
        peer = lax.rem(rank + i, N)
        pl.semaphore_signal(
            barrier, inc=1,
            device_id={"expert": peer // 2, "replica": lax.rem(peer, 2)}, device_id_type=MESH,
        )

    kcopies = []
    for b in range(S):
        kcopies.append(pltpu.make_async_copy(k_hbm.at[b], kb.at[pl.ds(b * L, L)], lsem.at[b]))
    vcopies = []
    for b in range(S):
        vcopies.append(pltpu.make_async_copy(v_hbm.at[b], vb.at[pl.ds(b * L, L)], lsem.at[S + b]))
    for cp in kcopies + vcopies:
        cp.start()
    orow = ow_hbm.shape[0]
    drow = wd_hbm.shape[1]
    omine = pl.ds(pl.multiple_of(c * orow, orow), orow)
    dmine = pl.ds(pl.multiple_of(c * drow, drow), drow)
    wcopies = [
        pltpu.make_async_copy(ow_hbm.at[:, mine], ow.at[omine], wsem.at[0]),
        pltpu.make_async_copy(wg_hbm.at[0], wg, wsem.at[1]),
        pltpu.make_async_copy(wu_hbm.at[0], wu, wsem.at[2]),
        pltpu.make_async_copy(wd_hbm.at[0, :, mine], wd.at[dmine], wsem.at[3]),
    ]
    for cp in wcopies:
        cp.start()

    for cp in small:
        cp.wait()
    qf = q_ref[...].astype(F32)
    for h in range(heads):
        qs[pl.ds(S * h, S), :] = qf[:, h * HEAD_WIDTH:(h + 1) * HEAD_WIDTH]
    for rep in range(8 // S):
        tks[pl.ds(rep * S, S), :] = tk_ref[...].astype(F32)
        tvs[pl.ds(rep * S, S), :] = tv_ref[...].astype(F32)
        resb[pl.ds(rep * S, S), :] = res_ref[...].astype(F32)
    rows = S * width
    row = lax.broadcasted_iota(jnp.int32, (rows, S * L), 0)
    col = lax.broadcasted_iota(jnp.int32, (rows, S * L), 1)
    seq = col // L
    length = jnp.zeros((rows, S * L), jnp.int32)
    for b in range(S):
        length = jnp.where(seq == b, kv_ref[b], length)
    seen = (row % S == seq) & (col - seq * L < length)
    inv_root = 1.0 / math.sqrt(HEAD_WIDTH)
    for cp in kcopies + vcopies:
        cp.wait()
    for g in range(G):
        lanes = slice(g * HEAD_WIDTH, (g + 1) * HEAD_WIDTH)
        qg = qs[g * rows:(g + 1) * rows, :]
        score = lax.dot_general(
            qg.astype(BF16), kb[:, lanes], (((1,), (1,)), ((), ())), preferred_element_type=F32
        ) * inv_root
        score = jnp.where(seen, score, -jnp.inf)
        tk = tks[:, lanes]
        tv = tvs[:, lanes]
        fresh = jnp.sum(
            (qg.reshape(rows // 8, 8, HEAD_WIDTH) * tk[None]).reshape(rows, HEAD_WIDTH),
            axis=1, keepdims=True,
        ) * inv_root
        top = jnp.maximum(jnp.max(score, axis=1, keepdims=True), fresh)
        ex = jnp.exp(score - top)
        fex = jnp.exp(fresh - top)
        inv = 1.0 / (jnp.sum(ex, axis=1, keepdims=True) + fex)
        prob = (ex * inv).astype(BF16)
        fprob = (fex * inv).astype(BF16).astype(F32)
        o = dot(prob, vb[:, lanes])
        o = o + (
            fprob.reshape(rows // 8, 8, 1) * tv[None]
        ).reshape(rows, HEAD_WIDTH)
        per = hpc * S
        if per == TILE:
            att[g * rows:(g + 1) * rows, :] = o.astype(BF16)
        else:
            for j in range(rows // per):
                base = (g * (rows // per) + j) * TILE
                att[base:base + per, :] = o[j * per:(j + 1) * per].astype(BF16)

    pl.semaphore_wait(barrier, N - 1)

    def tile(ref, index):
        return ref.at[pl.ds(pl.multiple_of(index * TILE, TILE), TILE)]

    def partner_of(index, i, count, inbound):
        if count & (count - 1) == 0:
            return flipped(index, count - i, count.bit_length() - 1)
        return lax.rem(index + count - i, count) if inbound else lax.rem(index + i, count)

    def att_copy(i, inbound=False):
        peer = partner_of(rank, i, N, inbound)
        who = peer if inbound else rank
        return pltpu.make_async_remote_copy(
            src_ref=tile(att, peer // 2), dst_ref=tile(ratt, who),
            send_sem=s1.at[i], recv_sem=r1.at[who],
            device_id={"expert": peer // 2, "replica": lax.rem(peer, 2)}, device_id_type=MESH,
        )

    def piece(ref, index, k):
        wide = ref.shape[-1] // CHUNKS
        return ref.at[
            pl.ds(pl.multiple_of(index * TILE, TILE), TILE), pl.ds(k * wide, wide)
        ]

    def spread(src, dst, send, recv, k, i, inbound=False):
        peer = partner_of(e_me, i, E, inbound)
        who = peer if inbound else e_me
        return pltpu.make_async_remote_copy(
            src_ref=piece(src, peer, k), dst_ref=piece(dst, who, k),
            send_sem=send.at[k, i], recv_sem=recv.at[k, who],
            device_id={"expert": peer, "replica": c}, device_id_type=MESH,
        )

    def scatter(src, dst, send, recv, k, own):
        @pl.loop(1, E)
        def _(i):
            spread(src, dst, send, recv, k, i).start()

        cp = pltpu.make_async_copy(piece(src, e_me, k), piece(dst, e_me, k), osem.at[own, k])
        cp.start()
        return cp

    def gather(src, dst, send, recv, k, cp):
        cp.wait()

        @pl.loop(1, E)
        def _(i):
            spread(src, dst, send, recv, k, i, True).wait_recv()

    def beside(src, dst, k):
        return pltpu.make_async_remote_copy(
            src_ref=src, dst_ref=dst, send_sem=psend.at[k], recv_sem=precv.at[k],
            device_id=partner, device_id_type=MESH,
        )

    ow_x = beside(ow_hbm.at[:, other], ow.at[omine], 0)
    wd_x = beside(wd_hbm.at[0, :, other], wd.at[dmine], 1)
    res_x = beside(resb.at[:, other], resp, 2)
    ow_x.start()

    @pl.loop(1, N)
    def _(i):
        att_copy(i).start()

    own1 = pltpu.make_async_copy(tile(att, e_me), tile(ratt, rank), lsem.at[0])
    own1.start()
    res_x.start()
    wd_x.start()

    lanes_all = E * TILE
    lane = lax.broadcasted_iota(jnp.int32, (T, lanes_all), 1)
    tok = lax.broadcasted_iota(jnp.int32, (T, lanes_all), 0)
    le = lane // TILE
    lq = (lane // cap) % Q
    ls = lane % cap
    ids = ids_ref[...]
    rw = rw_ref[...]
    mix = rw / jnp.sum(rw, axis=1, keepdims=True)
    named = jnp.zeros((T, lanes_all), F32)
    weight = jnp.zeros((T, lanes_all), F32)
    for k in range(ids.shape[1]):
        hit = ids[:, k:k + 1] == le
        named = named + jnp.where(hit, 1.0, 0.0)
        weight = weight + jnp.where(hit, mix[:, k:k + 1], 0.0)
    before = jnp.zeros((T, lanes_all), F32)
    for t in range(T - 1):
        before = before + jnp.where(tok > t, named[t:t + 1, :], 0.0)
    chosen = jnp.where(before == ls.astype(F32), named, 0.0)
    weight = weight * chosen
    high = weight.astype(BF16).astype(F32)
    low = weight - high
    for p in range(Q):
        here = lq == p
        tts[p * T:(p + 1) * T, :] = jnp.where(here, chosen, 0.0)
        whi[p * T:(p + 1) * T, :] = jnp.where(here, high, 0.0)
        wlo[p * T:(p + 1) * T, :] = jnp.where(here, low, 0.0)

    wcopies[0].wait()
    ow_x.wait()
    own1.wait()

    @pl.loop(1, N)
    def _(i):
        att_copy(i, True).wait_recv()

    pa = regroup(hpc, S)
    for grp in range(N // 8):
        blk = dot(pa, ratt[grp * 8 * TILE:(grp + 1) * 8 * TILE, :]).astype(BF16)
        for h in range(hpc):
            asm[grp * 8 * S:(grp + 1) * 8 * S, h * HEAD_WIDTH:(h + 1) * HEAD_WIDTH] = (
                blk[h * 8 * S:(h + 1) * 8 * S]
            )
    quarter = half // 2
    step = quarter // CHUNKS
    own2 = []
    for j in range(CHUNKS):
        y0 = dot(asm[...], ow[:, j * step:(j + 1) * step])
        y1 = dot(asm[...], ow[:, quarter + j * step:quarter + (j + 1) * step])
        both = jnp.concatenate([y0.reshape(E, T, step), y1.reshape(E, T, step)], axis=1)
        yb[:, j * step:(j + 1) * step] = both.reshape(E * TILE, step).astype(BF16)
        own2.append(scatter(yb, rs, s2, r2, j, 0))
    res_x.wait()
    sums = []
    for j in range(CHUNKS):
        gather(yb, rs, s2, r2, j, own2[j])
        cols = slice(j * step, (j + 1) * step)
        total = rs[0:TILE, cols].astype(F32)
        for k in range(1, E):
            total = total + rs[k * TILE:(k + 1) * TILE, cols].astype(F32)
        sums.append(total)
    projected = jnp.concatenate([t[:T] for t in sums] + [t[T:] for t in sums], axis=1)
    trow = lax.broadcasted_iota(jnp.int32, (T, half), 0)
    own_token = trow // S == c
    hidden = jnp.where(own_token, resb[:, mine], resp[...]) + projected
    hs[...] = hidden
    square = jnp.sum(hidden * hidden, axis=1, keepdims=True)
    ssb[...] = jnp.broadcast_to(square, ssb.shape)
    ss_x = beside(ssb, ssp, 3)
    ss_x.start()
    scaled = hidden * gain_ref[mine].astype(F32).reshape(1, half)
    ss_x.wait()
    mean = (square + ssp[:, 0:1]) / D
    normed = scaled * lax.rsqrt(mean + 1e-06)
    stacked = jnp.concatenate([normed[:, p * cw:(p + 1) * cw] for p in range(Q)], axis=0)
    stacked = stacked.astype(BF16)
    table = tts[...].astype(BF16)
    wide = cw // CHUNKS
    own3 = []
    for k in range(CHUNKS):
        picked = lax.dot_general(
            table, stacked[:, k * wide:(k + 1) * wide], (((0,), (0,)), ((), ())),
            preferred_element_type=F32,
        )
        xb[:, k * wide:(k + 1) * wide] = picked.astype(BF16)
        own3.append(scatter(xb, xr.at[c], s3, r3, k, 1))
    for cp in wcopies[1:]:
        cp.wait()
    wd_x.wait()
    px = regroup(Q, cap)
    gc = 8 * cap
    gate = jnp.zeros((E * cap, wg.shape[1]), F32)
    up = gate
    forwards = []
    for turn in range(2):
        side = c if turn == 0 else 1 - c
        for k in range(CHUNKS):
            cols = slice(k * wide, (k + 1) * wide)
            if turn == 0:
                gather(xb, xr.at[c], s3, r3, k, own3[k])
                mid = xr.at[c, :, pl.ds(k * wide, wide)]
                forwards.append(beside(mid, mid, (4, 7)[k]))
                forwards[k].start()
            else:
                forwards[k].wait()
            for grp in range(E // 8):
                blk = dot(px, xr[side, grp * 8 * TILE:(grp + 1) * 8 * TILE, cols]).astype(BF16)
                for p in range(Q):
                    xs[turn, grp * gc:(grp + 1) * gc, p * cw + k * wide:p * cw + (k + 1) * wide] = (
                        blk[p * gc:(p + 1) * gc]
                    )
            for p in range(Q):
                start = p * cw + k * wide
                feats = pl.ds(pl.multiple_of(side * half + start, wide), wide)
                rows_in = xs[turn, :, start:start + wide]
                gate = gate + dot(rows_in, wg[feats, :])
                up = up + dot(rows_in, wu[feats, :])
    hid[c] = (gate / (1.0 + jnp.exp(-gate)) * up).astype(BF16)
    h_x = beside(hid.at[c], hid.at[c], 5)
    h_x.start()
    h_x.wait()
    pb = regroup(Q, cap, True)
    own4 = []
    for k in range(CHUNKS):
        mid = slice(k * wide, (k + 1) * wide)
        for p in range(Q):
            cols = slice(p * cw + k * wide, p * cw + (k + 1) * wide)
            o = dot(hid[0], wd[0:drow, cols]) + dot(hid[1], wd[drow:2 * drow, cols])
            o = o.astype(BF16)
            for grp in range(E // 8):
                os[grp * 8 * TILE + p * gc:grp * 8 * TILE + (p + 1) * gc, mid] = (
                    o[grp * gc:(grp + 1) * gc]
                )
        for grp in range(E // 8):
            part = slice(grp * 8 * TILE, (grp + 1) * 8 * TILE)
            zb[part, mid] = dot(pb, os[part, mid]).astype(BF16)
        own4.append(scatter(zb, zr, s4, r4, k, 2))
    parts = []
    for k in range(CHUNKS):
        mid = slice(k * wide, (k + 1) * wide)
        gather(zb, zr, s4, r4, k, own4[k])
        parts.append(
            dot(whi[...].astype(BF16), zr[:, mid]) + dot(wlo[...].astype(BF16), zr[:, mid])
        )
    moe = jnp.concatenate(parts, axis=1)
    updated = hs[...] + jnp.concatenate([moe[p * T:(p + 1) * T] for p in range(Q)], axis=1)
    ub[...] = updated
    u_x = beside(ub, up_, 6)
    u_x.start()
    first = c == 0
    out_ref[:, mine] = jnp.where(first, updated[:S], updated[S:]).astype(BF16)
    u_x.wait()
    got = up_[...]
    out_ref[:, other] = jnp.where(first, got[:S], got[S:]).astype(BF16)

    @pl.loop(1, N)
    def _(i):
        att_copy(i).wait_send()

    @pl.loop(1, E)
    def _(i):
        for k in range(CHUNKS):
            spread(yb, rs, s2, r2, k, i).wait_send()
            spread(xb, xr.at[c], s3, r3, k, i).wait_send()
            spread(zb, zr, s4, r4, k, i).wait_send()


def on_device(
    queries, token_keys, token_values, stored_keys, stored_values, kv_len, residual, out_weight,
    norm_gain, expert_ids, route_weight, w_gate, w_up, w_down,
):
    E = lax.axis_size("expert")
    N = 2 * E
    S, features = queries.shape
    T = 2 * S
    L = stored_keys.shape[1]
    KW = token_keys.shape[1]
    D = residual.shape[1]
    half = D // 2
    topk = expert_ids.shape[1]
    FH = w_gate.shape[2]
    cap = max(2, -(-(T * topk) // E))
    Q = TILE // cap
    cw = half // Q
    orow = out_weight.shape[0]
    vmem = pl.BlockSpec(memory_space=pltpu.VMEM)
    hbm = pl.BlockSpec(memory_space=pltpu.HBM)
    V = pltpu.VMEM
    dma = pltpu.SemaphoreType.DMA
    scratch = [
        V((S, features), BF16), V((S, KW), BF16), V((S, KW), BF16), pltpu.SMEM((S,), jnp.int32),
        V((S, D), BF16), V((D,), BF16), V(expert_ids.shape, jnp.int32), V(route_weight.shape, F32),
        V((S * L, KW), BF16), V((S * L, KW), BF16),
        V((2 * orow, half), BF16), V((D, FH), BF16), V((D, FH), BF16), V((2 * FH, half), BF16),
        V((S * features // HEAD_WIDTH, HEAD_WIDTH), F32), V((8, KW), F32), V((8, KW), F32),
        V((E * TILE, HEAD_WIDTH), BF16), V((N * TILE, HEAD_WIDTH), BF16),
        V((N * S, 2 * orow), BF16),
        V((E * TILE, half // 2), BF16), V((E * TILE, half // 2), BF16),
        V((T, D), F32), V((T, half), F32), V((T, half), F32), V((T, 128), F32), V((T, 128), F32),
        V((Q * T, E * TILE), F32), V((Q * T, E * TILE), F32), V((Q * T, E * TILE), F32),
        V((E * TILE, cw), BF16), V((2, E * TILE, cw), BF16), V((2, E * cap, half), BF16),
        V((2, E * cap, FH), BF16),
        V((E * TILE, cw), BF16), V((E * TILE, cw), BF16), V((E * TILE, cw), BF16),
        V((T, half), F32), V((T, half), F32),
        dma((2 * S,)), dma((3, CHUNKS)), dma((4,)), dma((8,)), dma((8,)), dma((8,)),
        dma((N,)), dma((N,)), *[dma((CHUNKS, E))] * 6,
    ]
    return pl.pallas_call(
        functools.partial(kernel, E, cap),
        out_shape=jax.ShapeDtypeStruct((S, D), BF16),
        in_specs=[hbm] * 14,
        out_specs=vmem,
        scratch_shapes=scratch,
        compiler_params=pltpu.CompilerParams(
            collective_id=0, has_side_effects=True, vmem_limit_bytes=67043328
        ),
    )(
        queries, token_keys, token_values, kv_len, residual, norm_gain, expert_ids,
        route_weight, stored_keys, stored_values, out_weight, w_gate, w_up, w_down,
    )


def solution(mesh):
    rows = P(("groups", "expert", "replica"), None)
    cube = P(("groups", "expert", "replica"), None, None)
    in_specs = (
        rows, rows, rows, cube, cube, P(("groups", "expert", "replica")), rows,
        P(("expert", "replica"), None), P(), P(("groups", "expert"), None),
        P(("groups", "expert"), None), P("expert", None, "replica"),
        P("expert", None, "replica"), P("expert", "replica", None),
    )
    return jax.shard_map(
        on_device, mesh=mesh, in_specs=in_specs, out_specs=rows, check_vma=False
    )
```

profile of v0, /device:TPU:0, one launch (start us, length us, event | category | flops | bytes accessed | tf_op | source)
XLA Modules:
  0.0 52.9 jit_solution(1963616420592121500)
XLA Ops:
  0.0 51.5 %shard_map.136 = bf16[4,4096]{1,0:T(4,128)(2,1)} custom-call(bf16[4,8192]{1,0:T(4,128)(2,1)} %q_hbm.1, bf16[4,512]{1,0:T(4,128)(2,1)} %tk_hbm.1, bf16[4,512]{1,0:T(4,128)(2,1)} %tv_hbm.1, s32[4]{0:T(128)} %kv_hbm.1, bf16[4,4096]{1,0:T(4,128)(2,1)} %res_hbm.1, bf16[4096]{0:T(1024)(128)(2,1)} %gain_hbm.1, s32[8,8]{1,0:T(8,128)} %ids_hbm.1, f32[8,8]{1,0:T(8,128)} %rw_hbm.1, ...), custom_call_target="tpu_custom_call" | custom-call | tf_op jit(solution)/shard_map/pallas_call | solution.py:440
  51.5 1.4 %copy.16 = bf16[4,4096]{1,0:T(4,128)(2,1)} copy(bf16[4,4096]{1,0:T(4,128)(2,1)} %shard_map.136) | data formatting | bytes 65536
where the time goes:
time: 53.1 us; the launch traced here: 52.9 us
  Pallas kernels  51.5 us (97%)
  local copies, waits for them, and re-layouts  1.39 us (3%)
    pallas_call x1, Pallas kernels, on_device(): pl.pallas_call(functools.partial(kernel, E, cap), out_shape=jax.ShapeDtyp...  51.5 us
    unnamed x1, local copies, waits for them, and re-layouts  1.39 us

commit v1 on v0

v1 whole, which is shorter than its diff:
```python
import functools
import math

import jax
import jax.numpy as jnp
from jax import lax
from jax.experimental import pallas as pl
from jax.experimental.pallas import tpu as pltpu
from jax.sharding import PartitionSpec as P

HEAD_WIDTH = 128
TILE = 16
MESH = pl.DeviceIdType.MESH
F32 = jnp.float32
BF16 = jnp.bfloat16


def permutation(size, source):
    a = lax.broadcasted_iota(jnp.int32, (size, 8 * TILE), 0)
    b = lax.broadcasted_iota(jnp.int32, (size, 8 * TILE), 1)
    return jnp.where(b == source(a), 1.0, 0.0).astype(BF16)


def heads_out(hpc, S):
    return permutation(
        8 * hpc * S,
        lambda a: ((a // S) % 8) * TILE + (a % S) * hpc + a // (8 * S),
    )


def parts_out(Q, cap):
    return permutation(
        8 * Q * cap,
        lambda a: ((a // cap) % 8) * TILE + (a // (8 * cap)) * cap + a % cap,
    )


def parts_in(Q, cap):
    return permutation(
        8 * Q * cap,
        lambda a: ((a % TILE) // cap) * 8 * cap + (a // TILE) * cap + a % cap,
    )


def dot(a, b):
    return jnp.dot(a, b, preferred_element_type=F32)


def kernel(
    E, I, cap,
    q_hbm, tk_hbm, tv_hbm, kv_hbm, res_hbm, gain_hbm, ids_hbm, rw_hbm,
    k_hbm, v_hbm, ow_hbm, wg_hbm, wu_hbm, wd_hbm,
    out_hbm,
    q_ref, tk_ref, tv_ref, kv_ref, res_ref, gain_ref, ids_ref, rw_ref,
    kb, vb, owo, ow, wg, wu, wd,
    qs, tks, tvs, attf, att, ratt, asm,
    ya, rsa, yb, rsb, zb, rsc,
    resb, resp, hs, tts, whi, wlo,
    xb, xr, xs, gus, gur, hid, zs, zr, ub, up_, outb,
    isem, ksem, wsem, outsem, psend, precv,
    s1, r1, sa, ra, sb, rb, sc, rc, sx, rx, sz, rz,
):
    N = 2 * E
    O = E // I
    bits = E.bit_length() - 1
    e_me = lax.axis_index("expert")
    c = lax.axis_index("replica")
    rank = e_me * 2 + c
    S = q_ref.shape[0]
    T = 2 * S
    heads = q_ref.shape[1] // HEAD_WIDTH
    G = tk_ref.shape[1] // HEAD_WIDTH
    width = heads // G
    L = k_hbm.shape[1]
    D = res_ref.shape[1]
    half = D // 2
    hpc = heads // E
    Q = TILE // cap
    wide = half // 2
    piece = wide // Q
    FH = wg_hbm.shape[2]
    orow = ow_hbm.shape[0]
    drow = wd_hbm.shape[1]
    mine = pl.ds(pl.multiple_of(c * half, half), half)
    other = pl.ds(pl.multiple_of((1 - c) * half, half), half)
    omine = pl.ds(pl.multiple_of(c * orow, orow), orow)
    dmine = pl.ds(pl.multiple_of(c * drow, drow), drow)
    fmine = pl.ds(pl.multiple_of(c * FH, FH), FH)

    place = []
    for k in range(bits):
        bit = lax.rem(lax.div(e_me, 1 << k), 2)
        place.append((bit * (1 << k), (1 - bit) * (1 << k)))

    def expert_at(mask):
        return functools.reduce(lambda a, b: a + b, [place[k][(mask >> k) & 1] for k in range(bits)])

    peer = [expert_at(m) for m in range(E)]
    side = [c, 1 - c]
    order = {m: (m % I) * O + m // I for m in range(E)}

    small = [
        pltpu.make_async_copy(src, dst, isem.at[k])
        for k, (src, dst) in enumerate((
            (q_hbm, q_ref), (tk_hbm, tk_ref), (tv_hbm, tv_ref), (kv_hbm, kv_ref),
            (res_hbm, res_ref), (gain_hbm, gain_ref), (ids_hbm, ids_ref), (rw_hbm, rw_ref),
        ))
    ]
    kcopies = [
        pltpu.make_async_copy(k_hbm.at[b], kb.at[pl.ds(b * L, L)], ksem.at[b]) for b in range(S)
    ]
    vcopies = [
        pltpu.make_async_copy(v_hbm.at[b], vb.at[pl.ds(b * L, L)], ksem.at[S + b]) for b in range(S)
    ]
    wcopies = [
        pltpu.make_async_copy(ow_hbm.at[:, other], owo, wsem.at[0]),
        pltpu.make_async_copy(ow_hbm.at[:, mine], ow.at[omine], wsem.at[1]),
        pltpu.make_async_copy(wg_hbm.at[0, mine], wg.at[:, fmine], wsem.at[2]),
        pltpu.make_async_copy(wu_hbm.at[0, mine], wu.at[:, fmine], wsem.at[3]),
        pltpu.make_async_copy(wd_hbm.at[0, :, mine], wd.at[dmine], wsem.at[4]),
    ]
    for cp in small[:4] + kcopies + vcopies:
        cp.start()
    barrier = pltpu.get_barrier_semaphore()
    for m in range(E - 1, -1, -1):
        for k in (0, 1):
            if m or k:
                pl.semaphore_signal(
                    barrier, inc=1,
                    device_id={"expert": peer[m], "replica": side[k]}, device_id_type=MESH,
                )
    for cp in small[4:]:
        cp.start()

    for cp in small[:4]:
        cp.wait()
    qf = q_ref[...].astype(F32)
    for h in range(heads):
        qs[pl.ds(S * h, S), :] = qf[:, h * HEAD_WIDTH:(h + 1) * HEAD_WIDTH]
    tks[0:S, :] = tk_ref[...].astype(F32)
    tvs[0:S, :] = tv_ref[...].astype(F32)
    if hpc * S < TILE:
        attf[...] = jnp.zeros_like(attf)
    inv_root = 1.0 / math.sqrt(HEAD_WIDTH)
    group = lax.broadcasted_iota(jnp.int32, (heads, HEAD_WIDTH), 0) // width
    col = lax.broadcasted_iota(jnp.int32, (heads, L), 1)

    def by_head(ref, b):
        return jnp.concatenate([
            jnp.broadcast_to(ref[b:b + 1, g * HEAD_WIDTH:(g + 1) * HEAD_WIDTH], (width, HEAD_WIDTH))
            for g in range(G)
        ], axis=0)

    rows_q = []
    fresh = []
    for b in range(S):
        qb = qs[pl.ds(b, heads, stride=S), :]
        rows_q.append(jnp.concatenate(
            [jnp.where(group == g, qb, 0.0).astype(BF16) for g in range(G)], axis=1
        ))
        fresh.append(jnp.sum(qb * by_head(tks, b), axis=1, keepdims=True) * inv_root)
    for cp in kcopies:
        cp.wait()
    probs = []
    fprobs = []
    for b in range(S):
        score = lax.dot_general(
            rows_q[b], kb[b * L:(b + 1) * L, :], (((1,), (1,)), ((), ())),
            preferred_element_type=F32,
        ) * inv_root
        score = jnp.where(col < kv_ref[b], score, -jnp.inf)
        top = jnp.maximum(jnp.max(score, axis=1, keepdims=True), fresh[b])
        ex = jnp.exp(score - top)
        fex = jnp.exp(fresh[b] - top)
        inv = 1.0 / (jnp.sum(ex, axis=1, keepdims=True) + fex)
        probs.append((ex * inv).astype(BF16))
        fprobs.append((fex * inv).astype(BF16).astype(F32))
    for cp in vcopies:
        cp.wait()
    for cp in wcopies:
        cp.start()
    for b in range(S):
        o = dot(probs[b], vb[b * L:(b + 1) * L, :])
        o = jnp.concatenate([
            o[g * width:(g + 1) * width, g * HEAD_WIDTH:(g + 1) * HEAD_WIDTH] for g in range(G)
        ], axis=0)
        o = o + fprobs[b] * by_head(tvs, b)
        for j in range(E):
            attf[j * TILE + b * hpc:j * TILE + (b + 1) * hpc, :] = o[j * hpc:(j + 1) * hpc]
    att[...] = attf[...].astype(BF16)

    pl.semaphore_wait(barrier, N - 1)

    def rows_at(start, count):
        return pl.ds(pl.multiple_of(start * TILE, TILE), count * TILE)

    def att_copy(m, k):
        return pltpu.make_async_remote_copy(
            src_ref=att.at[rows_at(peer[m], 1)], dst_ref=ratt.at[rows_at(2 * order[m] + c, 1)],
            send_sem=s1.at[2 * m + k], recv_sem=r1.at[2 * m + k],
            device_id={"expert": peer[m], "replica": side[k]}, device_id_type=MESH,
        )

    def to_peer(src, dst, send, recv, m):
        return pltpu.make_async_remote_copy(
            src_ref=src, dst_ref=dst, send_sem=send, recv_sem=recv,
            device_id={"expert": peer[m], "replica": c}, device_id_type=MESH,
        )

    def beside(src, dst, k):
        return pltpu.make_async_remote_copy(
            src_ref=src, dst_ref=dst, send_sem=psend.at[k], recv_sem=precv.at[k],
            device_id={"expert": e_me, "replica": 1 - c}, device_id_type=MESH,
        )

    far_first = range(E - 1, 0, -1)
    att_x = [att_copy(m, k) for m in far_first for k in (0, 1)] + [att_copy(0, 1)]
    for cp in att_x:
        cp.start()
    wcopies[0].wait()
    ow_x = beside(owo, ow.at[omine], 0)
    ow_x.start()
    for cp in small[4:]:
        cp.wait()
    ratt[rows_at(c, 1)] = att[rows_at(e_me, 1)]
    for rep in range(8 // S):
        resb[pl.ds(rep * S, S), :] = res_ref[...].astype(F32)
    res_x = beside(resb.at[:, other], resp, 1)
    res_x.start()

    lanes_all = E * TILE
    lane = lax.broadcasted_iota(jnp.int32, (T, lanes_all), 1)
    tok = lax.broadcasted_iota(jnp.int32, (T, lanes_all), 0)
    lm = lane // TILE
    le = jnp.zeros((T, lanes_all), jnp.int32)
    for k in range(bits):
        flip = (lm // (1 << k)) % 2
        le = le + jnp.where(flip == 1, place[k][1], place[k][0])
    lq = (lane // cap) % Q
    ls = lane % cap
    ids = ids_ref[...]
    rw = rw_ref[...]
    mix = rw / jnp.sum(rw, axis=1, keepdims=True)
    named = jnp.zeros((T, lanes_all), F32)
    weight = jnp.zeros((T, lanes_all), F32)
    for k in range(ids.shape[1]):
        hit = ids[:, k:k + 1] == le
        named = named + jnp.where(hit, 1.0, 0.0)
        weight = weight + jnp.where(hit, mix[:, k:k + 1], 0.0)
    before = jnp.zeros((T, lanes_all), F32)
    for t in range(T - 1):
        before = before + jnp.where(tok > t, named[t:t + 1, :], 0.0)
    chosen = jnp.where(before == ls.astype(F32), named, 0.0)
    weight = weight * chosen
    high = weight.astype(BF16).astype(F32)
    low = weight - high
    for p in range(Q):
        here = lq == p
        tts[p * T:(p + 1) * T, :] = jnp.where(here, chosen, 0.0)
        whi[p * T:(p + 1) * T, :] = jnp.where(here, high, 0.0)
        wlo[p * T:(p + 1) * T, :] = jnp.where(here, low, 0.0)

    wcopies[1].wait()
    ow_x.wait()
    for cp in att_x:
        cp.wait_recv()

    pa = heads_out(hpc, S)
    for grp in range(N // 8):
        blk = dot(pa, ratt[grp * 8 * TILE:(grp + 1) * 8 * TILE, :]).astype(BF16)
        for h in range(hpc):
            asm[grp * 8 * S:(grp + 1) * 8 * S, h * HEAD_WIDTH:(h + 1) * HEAD_WIDTH] = (
                blk[h * 8 * S:(h + 1) * 8 * S]
            )
    lanes = wide // 2

    def project(chunk):
        y = [
            dot(asm[...], ow[:, chunk * wide + j * lanes:chunk * wide + (j + 1) * lanes])
            for j in (0, 1)
        ]
        both = jnp.concatenate([v.reshape(E, T, lanes) for v in y], axis=1)
        return both.reshape(E * TILE, lanes).astype(BF16)

    inner = range(1, I)
    outer = range(1, O)
    yb[...] = project(1)
    b_x = [
        to_peer(yb.at[rows_at(p * O, O)], rsb.at[p], sb.at[p], rb.at[p], p) for p in inner
    ]
    for cp in b_x:
        cp.start()
    ya[...] = project(0)
    a_x = [
        to_peer(
            ya.at[rows_at(order[m], 1)], rsa.at[rows_at(order[m], 1)], sa.at[m], ra.at[m], m
        )
        for m in far_first
    ]
    for cp in a_x:
        cp.start()
    wg_x = beside(wg_hbm.at[0, other], wg.at[:, fmine], 2)
    wu_x = beside(wu_hbm.at[0, other], wu.at[:, fmine], 3)
    wd_x = beside(wd_hbm.at[0, :, other], wd.at[dmine], 4)
    for cp in (wg_x, wu_x, wd_x):
        cp.start()

    for cp in b_x:
        cp.wait_recv()
    relay = yb[0:O * TILE, :].astype(F32)
    for p in inner:
        relay = relay + rsb[p].astype(F32)
    zb[...] = relay.astype(BF16)
    c_x = [
        to_peer(zb.at[rows_at(o, 1)], rsc.at[rows_at(o, 1)], sc.at[o], rc.at[o], o * I)
        for o in reversed(outer)
    ]
    for cp in c_x:
        cp.start()
    kept = relay[0:TILE]

    res_x.wait()
    for cp in att_x:
        cp.wait_send()
    trow = lax.broadcasted_iota(jnp.int32, (T, half), 0)
    base = jnp.where(trow // S == c, resb[:, mine], resp[...])
    table = tts[...].astype(BF16)

    def dispatch(chunk, total):
        hidden = base[:, chunk * wide:(chunk + 1) * wide] + jnp.concatenate(
            [total[:T], total[T:]], axis=1
        )
        hs[:, chunk * wide:(chunk + 1) * wide] = hidden
        stacked = jnp.concatenate(
            [hidden[:, p * piece:(p + 1) * piece] for p in range(Q)], axis=0
        ).astype(BF16)
        picked = lax.dot_general(
            table, stacked, (((0,), (0,)), ((), ())), preferred_element_type=F32
        ).astype(BF16)
        xb[chunk] = picked
        copies = [
            to_peer(
                xb.at[chunk, rows_at(m, 1)], xr.at[chunk, rows_at(m, 1)],
                sx.at[chunk, m], rx.at[chunk, m], m,
            )
            for m in far_first
        ]
        for cp in copies:
            cp.start()
        xr[chunk, 0:TILE] = picked[0:TILE]
        return copies

    for cp in a_x:
        cp.wait_recv()
    total = ya[0:TILE, :].astype(F32)
    for m in range(1, E):
        total = total + rsa[m * TILE:(m + 1) * TILE, :].astype(F32)
    x_x = [dispatch(0, total)]
    for cp in c_x:
        cp.wait_recv()
    total = kept
    for o in outer:
        total = total + rsc[o * TILE:(o + 1) * TILE, :].astype(F32)
    x_x.append(dispatch(1, total))

    for cp in wcopies[2:]:
        cp.wait()
    wg_x.wait()
    wu_x.wait()
    wd_x.wait()
    for cp in a_x + b_x + c_x:
        cp.wait_send()
    px = parts_out(Q, cap)
    gc = 8 * cap
    rows = E * cap
    gain = gain_ref[mine].astype(F32).reshape(1, half)
    square = jnp.zeros((rows, 1), F32)
    F = 2 * FH
    for k in range(2):
        for cp in x_x[k]:
            cp.wait_recv()
        blk = [
            dot(px, xr[k, grp * 8 * TILE:(grp + 1) * 8 * TILE, :]) for grp in range(E // 8)
        ]
        for p in range(Q):
            part = jnp.concatenate([v[p * gc:(p + 1) * gc] for v in blk], axis=0)
            square = square + jnp.sum(part * part, axis=1, keepdims=True)
            cols = slice(k * wide + p * piece, k * wide + (p + 1) * piece)
            xs[:, cols] = (part * gain[:, cols]).astype(BF16)
        feats = slice(k * wide, (k + 1) * wide)
        if k == 0:
            gus[:, 128:128 + F] = dot(xs[:, feats], wg[feats, :])
            gus[:, 128 + F:128 + 2 * F] = dot(xs[:, feats], wu[feats, :])
        else:
            gus[:, 0:128] = jnp.broadcast_to(square, (rows, 128))
            gus[:, 128:128 + F] += dot(xs[:, feats], wg[feats, :])
            first = pl.ds(0, 128 + F)
            g_x = beside(gus.at[:, first], gur.at[:, first], 5)
            g_x.start()
            gus[:, 128 + F:128 + 2 * F] += dot(xs[:, feats], wu[feats, :])
            second = pl.ds(128 + F, F)
            u_x = beside(gus.at[:, second], gur.at[:, second], 6)
            u_x.start()
    g_x.wait()
    scale = lax.rsqrt((gus[:, 0:1] + gur[:, 0:1]) / D + 1e-06)
    gate = (gus[:, 128:128 + F] + gur[:, 128:128 + F]) * scale
    gate = gate / (1.0 + jnp.exp(-gate))
    u_x.wait()
    up = (gus[:, 128 + F:128 + 2 * F] + gur[:, 128 + F:128 + 2 * F]) * scale
    hid[...] = (gate * up).astype(BF16)

    pb = parts_in(Q, cap)
    z_x = []
    for k in range(2):
        o = dot(hid[...], wd[:, k * wide:(k + 1) * wide]).astype(BF16)
        for grp in range(E // 8):
            blk = jnp.concatenate([
                o[grp * gc:(grp + 1) * gc, p * piece:(p + 1) * piece] for p in range(Q)
            ], axis=0)
            zs[k, grp * 8 * TILE:(grp + 1) * 8 * TILE, :] = dot(pb, blk).astype(BF16)
        copies = [
            to_peer(
                zs.at[k, rows_at(m, 1)], zr.at[k, rows_at(m, 1)], sz.at[k, m], rz.at[k, m], m
            )
            for m in far_first
        ]
        for cp in copies:
            cp.start()
        zr[k, 0:TILE] = zs[k, 0:TILE]
        z_x.append(copies)

    for k in range(2):
        for cp in x_x[k]:
            cp.wait_send()
    wh = whi[...].astype(BF16)
    wl = wlo[...].astype(BF16)
    own = c == 0
    f_x = []
    for k in range(2):
        for cp in z_x[k]:
            cp.wait_recv()
        part = dot(wh, zr[k]) + dot(wl, zr[k])
        cols = slice(k * wide, (k + 1) * wide)
        updated = hs[:, cols] + jnp.concatenate(
            [part[p * T:(p + 1) * T] for p in range(Q)], axis=1
        )
        ub[:, cols] = updated
        f_x.append(beside(ub.at[:, pl.ds(k * wide, wide)], up_.at[:, pl.ds(k * wide, wide)], 7 + k))
        f_x[k].start()
        at = pl.ds(pl.multiple_of(c * half + k * wide, wide), wide)
        outb[:, at] = jnp.where(own, updated[:S], updated[S:]).astype(BF16)
    outs = [pltpu.make_async_copy(outb.at[:, mine], out_hbm.at[:, mine], outsem.at[0])]
    outs[0].start()
    for k in range(2):
        for cp in z_x[k]:
            cp.wait_send()
    for cp in f_x:
        cp.wait()
    got = up_[...]
    outb[:, other] = jnp.where(own, got[:S], got[S:]).astype(BF16)
    outs.append(pltpu.make_async_copy(outb.at[:, other], out_hbm.at[:, other], outsem.at[1]))
    outs[1].start()
    for cp in outs:
        cp.wait()


def on_device(
    queries, token_keys, token_values, stored_keys, stored_values, kv_len, residual, out_weight,
    norm_gain, expert_ids, route_weight, w_gate, w_up, w_down,
):
    E = lax.axis_size("expert")
    N = 2 * E
    I = 1 << ((E.bit_length() - 1) // 2)
    O = E // I
    S, features = queries.shape
    T = 2 * S
    L = stored_keys.shape[1]
    KW = token_keys.shape[1]
    D = residual.shape[1]
    half = D // 2
    wide = half // 2
    topk = expert_ids.shape[1]
    FH = w_gate.shape[2]
    cap = max(2, -(-(T * topk) // E))
    Q = TILE // cap
    piece = wide // Q
    orow = out_weight.shape[0]
    hbm = pl.BlockSpec(memory_space=pltpu.HBM)
    V = pltpu.VMEM
    dma = pltpu.SemaphoreType.DMA
    wout = 128 + 4 * FH
    scratch = [
        V((S, features), BF16), V((S, KW), BF16), V((S, KW), BF16), pltpu.SMEM((S,), jnp.int32),
        V((S, D), BF16), V((D,), BF16), V(expert_ids.shape, jnp.int32), V(route_weight.shape, F32),
        V((S * L, KW), BF16), V((S * L, KW), BF16),
        V((orow, half), BF16), V((2 * orow, half), BF16),
        V((half, 2 * FH), BF16), V((half, 2 * FH), BF16), V((2 * FH, half), BF16),
        V((S * features // HEAD_WIDTH, HEAD_WIDTH), F32), V((8, KW), F32), V((8, KW), F32),
        V((E * TILE, HEAD_WIDTH), F32), V((E * TILE, HEAD_WIDTH), BF16),
        V((N * TILE, HEAD_WIDTH), BF16), V((N * S, 2 * orow), BF16),
        V((E * TILE, wide // 2), BF16), V((E * TILE, wide // 2), BF16),
        V((E * TILE, wide // 2), BF16), V((I, O * TILE, wide // 2), BF16),
        V((O * TILE, wide // 2), BF16), V((O * TILE, wide // 2), BF16),
        V((T, D), F32), V((T, half), F32), V((T, half), F32),
        V((Q * T, E * TILE), F32), V((Q * T, E * TILE), F32), V((Q * T, E * TILE), F32),
        V((2, E * TILE, piece), BF16), V((2, E * TILE, piece), BF16), V((E * cap, half), BF16),
        V((E * cap, wout), F32), V((E * cap, wout), F32), V((E * cap, 2 * FH), BF16),
        V((2, E * TILE, piece), BF16), V((2, E * TILE, piece), BF16),
        V((T, half), F32), V((T, half), F32), V((S, D), BF16),
        dma((8,)), dma((2 * S,)), dma((5,)), dma((2,)), dma((9,)), dma((9,)),
        dma((N,)), dma((N,)), dma((E,)), dma((E,)), dma((I,)), dma((I,)), dma((O,)), dma((O,)),
        dma((2, E)), dma((2, E)), dma((2, E)), dma((2, E)),
    ]
    return pl.pallas_call(
        functools.partial(kernel, E, I, cap),
        out_shape=jax.ShapeDtypeStruct((S, D), BF16),
        in_specs=[hbm] * 14,
        out_specs=hbm,
        scratch_shapes=scratch,
        compiler_params=pltpu.CompilerParams(
            collective_id=0, has_side_effects=True, vmem_limit_bytes=67043328
        ),
    )(
        queries, token_keys, token_values, kv_len, residual, norm_gain, expert_ids,
        route_weight, stored_keys, stored_values, out_weight, w_gate, w_up, w_down,
    )


def solution(mesh):
    rows = P(("groups", "expert", "replica"), None)
    cube = P(("groups", "expert", "replica"), None, None)
    in_specs = (
        rows, rows, rows, cube, cube, P(("groups", "expert", "replica")), rows,
        P(("expert", "replica"), None), P(), P(("groups", "expert"), None),
        P(("groups", "expert"), None), P("expert", None, "replica"),
        P("expert", None, "replica"), P("expert", "replica", None),
    )
    return jax.shard_map(
        on_device, mesh=mesh, in_specs=in_specs, out_specs=rows, check_vma=False
    )
```

time: 53.1 us -> 46.1 us (0.87)
  Pallas kernels: 51.5 us -> 44.5 us
    pallas_call x1, Pallas kernels: 51.5 us -> 44.5 us  [on_device(): pl.pallas_call(functools.partial(kernel, E, I, cap), out_shape=jax.ShapeD...]
where the time goes in v1:
time: 46.1 us; the launch traced here: 45.9 us
  Pallas kernels  44.5 us (97%)
  local copies, waits for them, and re-layouts  1.39 us (3%)
    pallas_call x1, Pallas kernels, on_device(): pl.pallas_call(functools.partial(kernel, E, I, cap), out_shape=jax.ShapeD...  44.5 us
    unnamed x1, local copies, waits for them, and re-layouts  1.39 us

profile of v1, /device:TPU:0, one launch (start us, length us, event | category | flops | bytes accessed | tf_op | source)
XLA Modules:
  0.0 45.9 jit_solution(1925639440870135258)
XLA Ops:
  0.0 44.5 %shard_map.136 = bf16[4,4096]{1,0:T(4,128)(2,1)} custom-call(bf16[4,8192]{1,0:T(4,128)(2,1)} %q_hbm.1, bf16[4,512]{1,0:T(4,128)(2,1)} %tk_hbm.1, bf16[4,512]{1,0:T(4,128)(2,1)} %tv_hbm.1, s32[4]{0:T(128)} %kv_hbm.1, bf16[4,4096]{1,0:T(4,128)(2,1)} %res_hbm.1, bf16[4096]{0:T(1024)(128)(2,1)} %gain_hbm.1, s32[8,8]{1,0:T(8,128)} %ids_hbm.1, f32[8,8]{1,0:T(8,128)} %rw_hbm.1, ...), custom_call_target="tpu_custom_call" | custom-call | tf_op jit(solution)/shard_map/pallas_call | solution.py:514
  44.5 1.4 %copy.16 = bf16[4,4096]{1,0:T(4,128)(2,1)} copy(bf16[4,4096]{1,0:T(4,128)(2,1)} %shard_map.136) | data formatting | bytes 65536

commit v2 on v1

--- a/solution.py
+++ b/solution.py
@@ -50,14 +50,14 @@
     E, I, cap,
     q_hbm, tk_hbm, tv_hbm, kv_hbm, res_hbm, gain_hbm, ids_hbm, rw_hbm,
     k_hbm, v_hbm, ow_hbm, wg_hbm, wu_hbm, wd_hbm,
-    out_hbm,
+    out_ref,
     q_ref, tk_ref, tv_ref, kv_ref, res_ref, gain_ref, ids_ref, rw_ref,
     kb, vb, owo, ow, wg, wu, wd,
     qs, tks, tvs, attf, att, ratt, asm,
     ya, rsa, yb, rsb, zb, rsc,
     resb, resp, hs, tts, whi, wlo,
-    xb, xr, xs, gus, gur, hid, zs, zr, ub, up_, outb,
-    isem, ksem, wsem, outsem, psend, precv,
+    xb, xr, xs, gus, gur, hid, zs, zr, ub, up_,
+    isem, ksem, wsem, psend, precv,
     s1, r1, sa, ra, sb, rb, sc, rc, sx, rx, sz, rz,
 ):
     N = 2 * E
@@ -77,7 +77,9 @@
     hpc = heads // E
     Q = TILE // cap
     wide = half // 2
-    piece = wide // Q
+    piece = HEAD_WIDTH
+    step = Q * piece
+    C = half // step
     FH = wg_hbm.shape[2]
     orow = ow_hbm.shape[0]
     drow = wd_hbm.shape[1]
@@ -106,12 +108,8 @@
             (res_hbm, res_ref), (gain_hbm, gain_ref), (ids_hbm, ids_ref), (rw_hbm, rw_ref),
         ))
     ]
-    kcopies = [
-        pltpu.make_async_copy(k_hbm.at[b], kb.at[pl.ds(b * L, L)], ksem.at[b]) for b in range(S)
-    ]
-    vcopies = [
-        pltpu.make_async_copy(v_hbm.at[b], vb.at[pl.ds(b * L, L)], ksem.at[S + b]) for b in range(S)
-    ]
+    k_copy = pltpu.make_async_copy(k_hbm, kb, ksem.at[0])
+    v_copy = pltpu.make_async_copy(v_hbm, vb, ksem.at[1])
     wcopies = [
         pltpu.make_async_copy(ow_hbm.at[:, other], owo, wsem.at[0]),
         pltpu.make_async_copy(ow_hbm.at[:, mine], ow.at[omine], wsem.at[1]),
@@ -119,7 +117,7 @@
         pltpu.make_async_copy(wu_hbm.at[0, mine], wu.at[:, fmine], wsem.at[3]),
         pltpu.make_async_copy(wd_hbm.at[0, :, mine], wd.at[dmine], wsem.at[4]),
     ]
-    for cp in small[:4] + kcopies + vcopies:
+    for cp in small[:4] + [k_copy, v_copy]:
         cp.start()
     barrier = pltpu.get_barrier_semaphore()
     for m in range(E - 1, -1, -1):
@@ -159,13 +157,12 @@
             [jnp.where(group == g, qb, 0.0).astype(BF16) for g in range(G)], axis=1
         ))
         fresh.append(jnp.sum(qb * by_head(tks, b), axis=1, keepdims=True) * inv_root)
-    for cp in kcopies:
-        cp.wait()
+    k_copy.wait()
     probs = []
     fprobs = []
     for b in range(S):
         score = lax.dot_general(
-            rows_q[b], kb[b * L:(b + 1) * L, :], (((1,), (1,)), ((), ())),
+            rows_q[b], kb[b], (((1,), (1,)), ((), ())),
             preferred_element_type=F32,
         ) * inv_root
         score = jnp.where(col < kv_ref[b], score, -jnp.inf)
@@ -175,12 +172,11 @@
         inv = 1.0 / (jnp.sum(ex, axis=1, keepdims=True) + fex)
         probs.append((ex * inv).astype(BF16))
         fprobs.append((fex * inv).astype(BF16).astype(F32))
-    for cp in vcopies:
-        cp.wait()
+    v_copy.wait()
     for cp in wcopies:
         cp.start()
     for b in range(S):
-        o = dot(probs[b], vb[b * L:(b + 1) * L, :])
+        o = dot(probs[b], vb[b])
         o = jnp.concatenate([
             o[g * width:(g + 1) * width, g * HEAD_WIDTH:(g + 1) * HEAD_WIDTH] for g in range(G)
         ], axis=0)
@@ -197,7 +193,7 @@
     def att_copy(m, k):
         return pltpu.make_async_remote_copy(
             src_ref=att.at[rows_at(peer[m], 1)], dst_ref=ratt.at[rows_at(2 * order[m] + c, 1)],
-            send_sem=s1.at[2 * m + k], recv_sem=r1.at[2 * m + k],
+            send_sem=s1.at[0], recv_sem=r1.at[0],
             device_id={"expert": peer[m], "replica": side[k]}, device_id_type=MESH,
         )
 
@@ -213,10 +209,14 @@
             device_id={"expert": e_me, "replica": 1 - c}, device_id_type=MESH,
         )
 
+    def whole(ref, send, recv):
+        return to_peer(ref, ref, send, recv, E - 1)
+
     far_first = range(E - 1, 0, -1)
     att_x = [att_copy(m, k) for m in far_first for k in (0, 1)] + [att_copy(0, 1)]
     for cp in att_x:
         cp.start()
+    att_all = whole(ratt.at[rows_at(0, N - 1)], s1.at[0], r1.at[0])
     wcopies[0].wait()
     ow_x = beside(owo, ow.at[omine], 0)
     ow_x.start()
@@ -262,8 +262,7 @@
 
     wcopies[1].wait()
     ow_x.wait()
-    for cp in att_x:
-        cp.wait_recv()
+    att_all.wait_recv()
 
     pa = heads_out(hpc, S)
     for grp in range(N // 8):
@@ -286,14 +285,14 @@
     outer = range(1, O)
     yb[...] = project(1)
     b_x = [
-        to_peer(yb.at[rows_at(p * O, O)], rsb.at[p], sb.at[p], rb.at[p], p) for p in inner
+        to_peer(yb.at[rows_at(p * O, O)], rsb.at[p], sb.at[0], rb.at[0], p) for p in inner
     ]
     for cp in b_x:
         cp.start()
     ya[...] = project(0)
     a_x = [
         to_peer(
-            ya.at[rows_at(order[m], 1)], rsa.at[rows_at(order[m], 1)], sa.at[m], ra.at[m], m
+            ya.at[rows_at(order[m], 1)], rsa.at[rows_at(order[m], 1)], sa.at[0], ra.at[0], m
         )
         for m in far_first
     ]
@@ -305,14 +304,14 @@
     for cp in (wg_x, wu_x, wd_x):
         cp.start()
 
-    for cp in b_x:
-        cp.wait_recv()
+    b_all = whole(rsb.at[pl.ds(1, I - 1)], sb.at[0], rb.at[0])
+    b_all.wait_recv()
     relay = yb[0:O * TILE, :].astype(F32)
     for p in inner:
         relay = relay + rsb[p].astype(F32)
     zb[...] = relay.astype(BF16)
     c_x = [
-        to_peer(zb.at[rows_at(o, 1)], rsc.at[rows_at(o, 1)], sc.at[o], rc.at[o], o * I)
+        to_peer(zb.at[rows_at(o, 1)], rsc.at[rows_at(o, 1)], sc.at[0], rc.at[0], o * I)
         for o in reversed(outer)
     ]
     for cp in c_x:
@@ -320,55 +319,53 @@
     kept = relay[0:TILE]
 
     res_x.wait()
-    for cp in att_x:
-        cp.wait_send()
+    att_all.wait_send()
     trow = lax.broadcasted_iota(jnp.int32, (T, half), 0)
     base = jnp.where(trow // S == c, resb[:, mine], resp[...])
     table = tts[...].astype(BF16)
 
-    def dispatch(chunk, total):
-        hidden = base[:, chunk * wide:(chunk + 1) * wide] + jnp.concatenate(
-            [total[:T], total[T:]], axis=1
-        )
-        hs[:, chunk * wide:(chunk + 1) * wide] = hidden
-        stacked = jnp.concatenate(
-            [hidden[:, p * piece:(p + 1) * piece] for p in range(Q)], axis=0
-        ).astype(BF16)
-        picked = lax.dot_general(
-            table, stacked, (((0,), (0,)), ((), ())), preferred_element_type=F32
-        ).astype(BF16)
-        xb[chunk] = picked
-        copies = [
-            to_peer(
-                xb.at[chunk, rows_at(m, 1)], xr.at[chunk, rows_at(m, 1)],
-                sx.at[chunk, m], rx.at[chunk, m], m,
-            )
-            for m in far_first
-        ]
-        for cp in copies:
-            cp.start()
-        xr[chunk, 0:TILE] = picked[0:TILE]
-        return copies
-
-    for cp in a_x:
-        cp.wait_recv()
+    x_x = []
+
+    def dispatch(first, total):
+        total = jnp.concatenate([total[:T], total[T:]], axis=1)
+        for at in range(0, wide, step):
+            cols = slice(first + at, first + at + step)
+            hidden = base[:, cols] + total[:, at:at + step]
+            hs[:, cols] = hidden
+            stacked = jnp.concatenate(
+                [hidden[:, p * piece:(p + 1) * piece] for p in range(Q)], axis=0
+            ).astype(BF16)
+            picked = lax.dot_general(
+                table, stacked, (((0,), (0,)), ((), ())), preferred_element_type=F32
+            ).astype(BF16)
+            k = len(x_x)
+            xb[k] = picked
+            for m in far_first:
+                to_peer(
+                    xb.at[k, rows_at(m, 1)], xr.at[k, rows_at(m, 1)], sx.at[k], rx.at[k], m
+                ).start()
+            xr[k, 0:TILE] = picked[0:TILE]
+            x_x.append(whole(xr.at[k, rows_at(1, E - 1)], sx.at[k], rx.at[k]))
+
+    a_all = whole(rsa.at[rows_at(1, E - 1)], sa.at[0], ra.at[0])
+    a_all.wait_recv()
     total = ya[0:TILE, :].astype(F32)
     for m in range(1, E):
         total = total + rsa[m * TILE:(m + 1) * TILE, :].astype(F32)
-    x_x = [dispatch(0, total)]
-    for cp in c_x:
-        cp.wait_recv()
+    dispatch(0, total)
+    c_all = whole(rsc.at[rows_at(1, O - 1)], sc.at[0], rc.at[0])
+    c_all.wait_recv()
     total = kept
     for o in outer:
         total = total + rsc[o * TILE:(o + 1) * TILE, :].astype(F32)
-    x_x.append(dispatch(1, total))
+    dispatch(wide, total)
 
     for cp in wcopies[2:]:
         cp.wait()
     wg_x.wait()
     wu_x.wait()
     wd_x.wait()
-    for cp in a_x + b_x + c_x:
+    for cp in (a_all, b_all, c_all):
         cp.wait_send()
     px = parts_out(Q, cap)
     gc = 8 * cap
@@ -376,31 +373,34 @@
     gain = gain_ref[mine].astype(F32).reshape(1, half)
     square = jnp.zeros((rows, 1), F32)
     F = 2 * FH
-    for k in range(2):
-        for cp in x_x[k]:
-            cp.wait_recv()
+    gates, ups = slice(128, 128 + F), slice(128 + F, 128 + 2 * F)
+    for k in range(C):
+        x_x[k].wait_recv()
         blk = [
             dot(px, xr[k, grp * 8 * TILE:(grp + 1) * 8 * TILE, :]) for grp in range(E // 8)
         ]
         for p in range(Q):
             part = jnp.concatenate([v[p * gc:(p + 1) * gc] for v in blk], axis=0)
             square = square + jnp.sum(part * part, axis=1, keepdims=True)
-            cols = slice(k * wide + p * piece, k * wide + (p + 1) * piece)
+            cols = slice(k * step + p * piece, k * step + (p + 1) * piece)
             xs[:, cols] = (part * gain[:, cols]).astype(BF16)
-        feats = slice(k * wide, (k + 1) * wide)
+        feats = slice(k * step, (k + 1) * step)
         if k == 0:
-            gus[:, 128:128 + F] = dot(xs[:, feats], wg[feats, :])
-            gus[:, 128 + F:128 + 2 * F] = dot(xs[:, feats], wu[feats, :])
+            gus[:, gates] = dot(xs[:, feats], wg[feats, :])
         else:
+            gus[:, gates] += dot(xs[:, feats], wg[feats, :])
+        if k == C - 1:
             gus[:, 0:128] = jnp.broadcast_to(square, (rows, 128))
-            gus[:, 128:128 + F] += dot(xs[:, feats], wg[feats, :])
             first = pl.ds(0, 128 + F)
             g_x = beside(gus.at[:, first], gur.at[:, first], 5)
             g_x.start()
-            gus[:, 128 + F:128 + 2 * F] += dot(xs[:, feats], wu[feats, :])
-            second = pl.ds(128 + F, F)
-            u_x = beside(gus.at[:, second], gur.at[:, second], 6)
-            u_x.start()
+        if k == 0:
+            gus[:, ups] = dot(xs[:, feats], wu[feats, :])
+        else:
+            gus[:, ups] += dot(xs[:, feats], wu[feats, :])
+    second = pl.ds(128 + F, F)
+    u_x = beside(gus.at[:, second], gur.at[:, second], 6)
+    u_x.start()
     g_x.wait()
     scale = lax.rsqrt((gus[:, 0:1] + gur[:, 0:1]) / D + 1e-06)
     gate = (gus[:, 128:128 + F] + gur[:, 128:128 + F]) * scale
@@ -411,57 +411,44 @@
 
     pb = parts_in(Q, cap)
     z_x = []
-    for k in range(2):
-        o = dot(hid[...], wd[:, k * wide:(k + 1) * wide]).astype(BF16)
+    for k in range(C):
+        o = dot(hid[...], wd[:, k * step:(k + 1) * step]).astype(BF16)
         for grp in range(E // 8):
             blk = jnp.concatenate([
                 o[grp * gc:(grp + 1) * gc, p * piece:(p + 1) * piece] for p in range(Q)
             ], axis=0)
             zs[k, grp * 8 * TILE:(grp + 1) * 8 * TILE, :] = dot(pb, blk).astype(BF16)
-        copies = [
+        for m in far_first:
             to_peer(
-                zs.at[k, rows_at(m, 1)], zr.at[k, rows_at(m, 1)], sz.at[k, m], rz.at[k, m], m
-            )
-            for m in far_first
-        ]
-        for cp in copies:
-            cp.start()
+                zs.at[k, rows_at(m, 1)], zr.at[k, rows_at(m, 1)], sz.at[k], rz.at[k], m
+            ).start()
         zr[k, 0:TILE] = zs[k, 0:TILE]
-        z_x.append(copies)
-
-    for k in range(2):
-        for cp in x_x[k]:
-            cp.wait_send()
+        z_x.append(whole(zr.at[k, rows_at(1, E - 1)], sz.at[k], rz.at[k]))
+
+    for cp in x_x:
+        cp.wait_send()
     wh = whi[...].astype(BF16)
     wl = wlo[...].astype(BF16)
     own = c == 0
     f_x = []
-    for k in range(2):
-        for cp in z_x[k]:
-            cp.wait_recv()
+    for k in range(C):
+        z_x[k].wait_recv()
         part = dot(wh, zr[k]) + dot(wl, zr[k])
-        cols = slice(k * wide, (k + 1) * wide)
+        cols = slice(k * step, (k + 1) * step)
         updated = hs[:, cols] + jnp.concatenate(
             [part[p * T:(p + 1) * T] for p in range(Q)], axis=1
         )
         ub[:, cols] = updated
-        f_x.append(beside(ub.at[:, pl.ds(k * wide, wide)], up_.at[:, pl.ds(k * wide, wide)], 7 + k))
+        f_x.append(beside(ub.at[:, pl.ds(k * step, step)], up_.at[:, pl.ds(k * step, step)], 7 + k))
         f_x[k].start()
-        at = pl.ds(pl.multiple_of(c * half + k * wide, wide), wide)
-        outb[:, at] = jnp.where(own, updated[:S], updated[S:]).astype(BF16)
-    outs = [pltpu.make_async_copy(outb.at[:, mine], out_hbm.at[:, mine], outsem.at[0])]
-    outs[0].start()
-    for k in range(2):
-        for cp in z_x[k]:
-            cp.wait_send()
+        at = pl.ds(pl.multiple_of(c * half + k * step, step), step)
+        out_ref[:, at] = jnp.where(own, updated[:S], updated[S:]).astype(BF16)
+    for cp in z_x:
+        cp.wait_send()
     for cp in f_x:
         cp.wait()
     got = up_[...]
-    outb[:, other] = jnp.where(own, got[:S], got[S:]).astype(BF16)
-    outs.append(pltpu.make_async_copy(outb.at[:, other], out_hbm.at[:, other], outsem.at[1]))
-    outs[1].start()
-    for cp in outs:
-        cp.wait()
+    out_ref[:, other] = jnp.where(own, got[:S], got[S:]).astype(BF16)
 
 
 def on_device(
@@ -483,7 +470,8 @@
     FH = w_gate.shape[2]
     cap = max(2, -(-(T * topk) // E))
     Q = TILE // cap
-    piece = wide // Q
+    piece = HEAD_WIDTH
+    C = half // (Q * piece)
     orow = out_weight.shape[0]
     hbm = pl.BlockSpec(memory_space=pltpu.HBM)
     V = pltpu.VMEM
@@ -492,7 +480,7 @@
     scratch = [
         V((S, features), BF16), V((S, KW), BF16), V((S, KW), BF16), pltpu.SMEM((S,), jnp.int32),
         V((S, D), BF16), V((D,), BF16), V(expert_ids.shape, jnp.int32), V(route_weight.shape, F32),
-        V((S * L, KW), BF16), V((S * L, KW), BF16),
+        V((S, L, KW), BF16), V((S, L, KW), BF16),
         V((orow, half), BF16), V((2 * orow, half), BF16),
         V((half, 2 * FH), BF16), V((half, 2 * FH), BF16), V((2 * FH, half), BF16),
         V((S * features // HEAD_WIDTH, HEAD_WIDTH), F32), V((8, KW), F32), V((8, KW), F32),
@@ -503,22 +491,21 @@
         V((O * TILE, wide // 2), BF16), V((O * TILE, wide // 2), BF16),
         V((T, D), F32), V((T, half), F32), V((T, half), F32),
         V((Q * T, E * TILE), F32), V((Q * T, E * TILE), F32), V((Q * T, E * TILE), F32),
-        V((2, E * TILE, piece), BF16), V((2, E * TILE, piece), BF16), V((E * cap, half), BF16),
+        V((C, E * TILE, piece), BF16), V((C, E * TILE, piece), BF16), V((E * cap, half), BF16),
         V((E * cap, wout), F32), V((E * cap, wout), F32), V((E * cap, 2 * FH), BF16),
-        V((2, E * TILE, piece), BF16), V((2, E * TILE, piece), BF16),
-        V((T, half), F32), V((T, half), F32), V((S, D), BF16),
-        dma((8,)), dma((2 * S,)), dma((5,)), dma((2,)), dma((9,)), dma((9,)),
-        dma((N,)), dma((N,)), dma((E,)), dma((E,)), dma((I,)), dma((I,)), dma((O,)), dma((O,)),
-        dma((2, E)), dma((2, E)), dma((2, E)), dma((2, E)),
+        V((C, E * TILE, piece), BF16), V((C, E * TILE, piece), BF16),
+        V((T, half), F32), V((T, half), F32),
+        dma((8,)), dma((2,)), dma((5,)), dma((7 + C,)), dma((7 + C,)),
+        *[dma((1,))] * 8, *[dma((C,))] * 4,
     ]
     return pl.pallas_call(
         functools.partial(kernel, E, I, cap),
-        out_shape=jax.ShapeDtypeStruct((S, D), BF16),
+        out_shape=pltpu.VMEM((S, D), BF16),
         in_specs=[hbm] * 14,
-        out_specs=hbm,
+        out_specs=pl.BlockSpec(memory_space=pltpu.VMEM),
         scratch_shapes=scratch,
         compiler_params=pltpu.CompilerParams(
-            collective_id=0, has_side_effects=True, vmem_limit_bytes=67043328
+            collective_id=0, has_side_effects=True, vmem_limit_bytes=66977792
         ),
     )(
         queries, token_keys, token_values, kv_len, residual, norm_gain, expert_ids,

time: 46.1 us -> 42.4 us (0.920)
  Pallas kernels: 44.5 us -> 41.7 us
  local copies, waits for them, and re-layouts: 1.39 us -> 0.62 us
    pallas_call x1, Pallas kernels: 44.5 us -> 41.7 us  [on_device(): pl.pallas_call(functools.partial(kernel, E, I, cap), out_shape=pltpu.VMEM...]
    unnamed x1, local copies, waits for them, and re-layouts: 1.39 us -> 0.62 us
where the time goes in v2:
time: 42.4 us; the launch traced here: 42.3 us
  Pallas kernels  41.7 us (98%)
  local copies, waits for them, and re-layouts  0.62 us (1%)
    pallas_call x1, Pallas kernels, on_device(): pl.pallas_call(functools.partial(kernel, E, I, cap), out_shape=pltpu.VMEM...  41.7 us

profile of v2, /device:TPU:0, one launch (start us, length us, event | category | flops | bytes accessed | tf_op | source)
XLA Modules:
  0.0 42.3 jit_solution(13364746524265587572)
XLA Ops:
  0.0 41.7 %shard_map.136 = bf16[4,4096]{1,0:T(4,128)(2,1)S(1)} custom-call(bf16[4,8192]{1,0:T(4,128)(2,1)} %q_hbm.1, bf16[4,512]{1,0:T(4,128)(2,1)} %tk_hbm.1, bf16[4,512]{1,0:T(4,128)(2,1)} %tv_hbm.1, s32[4]{0:T(128)} %kv_hbm.1, bf16[4,4096]{1,0:T(4,128)(2,1)} %res_hbm.1, bf16[4096]{0:T(1024)(128)(2,1)} %gain_hbm.1, s32[8,8]{1,0:T(8,128)} %ids_hbm.1, f32[8,8]{1,0:T(8,128)} %rw_hbm.1, ...), custom_call_target="tpu_custom_call" | custom-call | tf_op jit(solution)/shard_map/pallas_call | solution.py:501
  41.7 0.6 %copy.16 = bf16[4,4096]{1,0:T(4,128)(2,1)} copy(bf16[4,4096]{1,0:T(4,128)(2,1)S(1)} %shard_map.136) | data formatting | bytes 65536

commit v3 on v2

--- a/solution.py
+++ b/solution.py
@@ -40,6 +40,10 @@
         8 * Q * cap,
         lambda a: ((a % TILE) // cap) * 8 * cap + (a // TILE) * cap + a % cap,
     )
+
+
+def send_order(C):
+    return list(range(C // 2, C)) + list(range(C // 2))
 
 
 def dot(a, b):
@@ -54,7 +58,7 @@
     q_ref, tk_ref, tv_ref, kv_ref, res_ref, gain_ref, ids_ref, rw_ref,
     kb, vb, owo, ow, wg, wu, wd,
     qs, tks, tvs, attf, att, ratt, asm,
-    ya, rsa, yb, rsb, zb, rsc,
+    ys, rsa, rsb, zb, rsc,
     resb, resp, hs, tts, whi, wlo,
     xb, xr, xs, gus, gur, hid, zs, zr, ub, up_,
     isem, ksem, wsem, psend, precv,
@@ -76,7 +80,6 @@
     half = D // 2
     hpc = heads // E
     Q = TILE // cap
-    wide = half // 2
     piece = HEAD_WIDTH
     step = Q * piece
     C = half // step
@@ -218,8 +221,13 @@
         cp.start()
     att_all = whole(ratt.at[rows_at(0, N - 1)], s1.at[0], r1.at[0])
     wcopies[0].wait()
+    wg_x = beside(wg_hbm.at[0, other], wg.at[:, fmine], 2)
+    wu_x = beside(wu_hbm.at[0, other], wu.at[:, fmine], 3)
+    wd_x = beside(wd_hbm.at[0, :, other], wd.at[dmine], 4)
     ow_x = beside(owo, ow.at[omine], 0)
     ow_x.start()
+    for cp in (wg_x, wu_x, wd_x):
+        cp.start()
     for cp in small[4:]:
         cp.wait()
     ratt[rows_at(c, 1)] = att[rows_at(e_me, 1)]
@@ -271,52 +279,43 @@
             asm[grp * 8 * S:(grp + 1) * 8 * S, h * HEAD_WIDTH:(h + 1) * HEAD_WIDTH] = (
                 blk[h * 8 * S:(h + 1) * 8 * S]
             )
-    lanes = wide // 2
-
-    def project(chunk):
+    lanes = step // 2
+    direct = C // 2
+    inner = range(I - 1, 0, -1)
+    outer = range(O - 1, 0, -1)
+    for k in send_order(C):
         y = [
-            dot(asm[...], ow[:, chunk * wide + j * lanes:chunk * wide + (j + 1) * lanes])
-            for j in (0, 1)
+            dot(asm[...], ow[:, k * step + j * lanes:k * step + (j + 1) * lanes]) for j in (0, 1)
         ]
         both = jnp.concatenate([v.reshape(E, T, lanes) for v in y], axis=1)
-        return both.reshape(E * TILE, lanes).astype(BF16)
-
-    inner = range(1, I)
-    outer = range(1, O)
-    yb[...] = project(1)
-    b_x = [
-        to_peer(yb.at[rows_at(p * O, O)], rsb.at[p], sb.at[0], rb.at[0], p) for p in inner
-    ]
-    for cp in b_x:
-        cp.start()
-    ya[...] = project(0)
-    a_x = [
-        to_peer(
-            ya.at[rows_at(order[m], 1)], rsa.at[rows_at(order[m], 1)], sa.at[0], ra.at[0], m
-        )
-        for m in far_first
-    ]
-    for cp in a_x:
-        cp.start()
-    wg_x = beside(wg_hbm.at[0, other], wg.at[:, fmine], 2)
-    wu_x = beside(wu_hbm.at[0, other], wu.at[:, fmine], 3)
-    wd_x = beside(wd_hbm.at[0, :, other], wd.at[dmine], 4)
-    for cp in (wg_x, wu_x, wd_x):
-        cp.start()
-
-    b_all = whole(rsb.at[pl.ds(1, I - 1)], sb.at[0], rb.at[0])
-    b_all.wait_recv()
-    relay = yb[0:O * TILE, :].astype(F32)
-    for p in inner:
-        relay = relay + rsb[p].astype(F32)
-    zb[...] = relay.astype(BF16)
-    c_x = [
-        to_peer(zb.at[rows_at(o, 1)], rsc.at[rows_at(o, 1)], sc.at[0], rc.at[0], o * I)
-        for o in reversed(outer)
-    ]
-    for cp in c_x:
-        cp.start()
-    kept = relay[0:TILE]
+        ys[k] = both.reshape(E * TILE, lanes).astype(BF16)
+        if k < direct:
+            for m in far_first:
+                to_peer(
+                    ys.at[k, rows_at(order[m], 1)], rsa.at[k, rows_at(order[m], 1)],
+                    sa.at[k], ra.at[k], m,
+                ).start()
+        else:
+            b = k - direct
+            for p in inner:
+                to_peer(
+                    ys.at[k, rows_at(p * O, O)], rsb.at[b, p], sb.at[b], rb.at[b], p
+                ).start()
+    a_x = [whole(rsa.at[k, rows_at(1, E - 1)], sa.at[k], ra.at[k]) for k in range(direct)]
+    b_x = [whole(rsb.at[b, pl.ds(1, I - 1)], sb.at[b], rb.at[b]) for b in range(C - direct)]
+    c_x = [whole(rsc.at[b, rows_at(1, O - 1)], sc.at[b], rc.at[b]) for b in range(C - direct)]
+    kept = []
+    for b in range(C - direct):
+        b_x[b].wait_recv()
+        relay = ys[direct + b, 0:O * TILE, :].astype(F32)
+        for p in range(1, I):
+            relay = relay + rsb[b, p].astype(F32)
+        zb[b] = relay.astype(BF16)
+        kept.append(relay[0:TILE])
+        for o in outer:
+            to_peer(
+                zb.at[b, rows_at(o, 1)], rsc.at[b, rows_at(o, 1)], sc.at[b], rc.at[b], o * I
+            ).start()
 
     res_x.wait()
     att_all.wait_send()
@@ -326,46 +325,43 @@
 
     x_x = []
 
-    def dispatch(first, total):
-        total = jnp.concatenate([total[:T], total[T:]], axis=1)
-        for at in range(0, wide, step):
-            cols = slice(first + at, first + at + step)
-            hidden = base[:, cols] + total[:, at:at + step]
-            hs[:, cols] = hidden
-            stacked = jnp.concatenate(
-                [hidden[:, p * piece:(p + 1) * piece] for p in range(Q)], axis=0
-            ).astype(BF16)
-            picked = lax.dot_general(
-                table, stacked, (((0,), (0,)), ((), ())), preferred_element_type=F32
-            ).astype(BF16)
-            k = len(x_x)
-            xb[k] = picked
-            for m in far_first:
-                to_peer(
-                    xb.at[k, rows_at(m, 1)], xr.at[k, rows_at(m, 1)], sx.at[k], rx.at[k], m
-                ).start()
-            xr[k, 0:TILE] = picked[0:TILE]
-            x_x.append(whole(xr.at[k, rows_at(1, E - 1)], sx.at[k], rx.at[k]))
-
-    a_all = whole(rsa.at[rows_at(1, E - 1)], sa.at[0], ra.at[0])
-    a_all.wait_recv()
-    total = ya[0:TILE, :].astype(F32)
-    for m in range(1, E):
-        total = total + rsa[m * TILE:(m + 1) * TILE, :].astype(F32)
-    dispatch(0, total)
-    c_all = whole(rsc.at[rows_at(1, O - 1)], sc.at[0], rc.at[0])
-    c_all.wait_recv()
-    total = kept
-    for o in outer:
-        total = total + rsc[o * TILE:(o + 1) * TILE, :].astype(F32)
-    dispatch(wide, total)
+    def dispatch(k, total):
+        cols = slice(k * step, (k + 1) * step)
+        hidden = base[:, cols] + jnp.concatenate([total[:T], total[T:]], axis=1)
+        hs[:, cols] = hidden
+        stacked = jnp.concatenate(
+            [hidden[:, p * piece:(p + 1) * piece] for p in range(Q)], axis=0
+        ).astype(BF16)
+        picked = lax.dot_general(
+            table, stacked, (((0,), (0,)), ((), ())), preferred_element_type=F32
+        ).astype(BF16)
+        xb[k] = picked
+        for m in far_first:
+            to_peer(
+                xb.at[k, rows_at(m, 1)], xr.at[k, rows_at(m, 1)], sx.at[k], rx.at[k], m
+            ).start()
+        xr[k, 0:TILE] = picked[0:TILE]
+        x_x.append(whole(xr.at[k, rows_at(1, E - 1)], sx.at[k], rx.at[k]))
+
+    for k in range(direct):
+        a_x[k].wait_recv()
+        total = ys[k, 0:TILE, :].astype(F32)
+        for m in range(1, E):
+            total = total + rsa[k, m * TILE:(m + 1) * TILE, :].astype(F32)
+        dispatch(k, total)
+    for b in range(C - direct):
+        c_x[b].wait_recv()
+        total = kept[b]
+        for o in range(1, O):
+            total = total + rsc[b, o * TILE:(o + 1) * TILE, :].astype(F32)
+        dispatch(direct + b, total)
 
     for cp in wcopies[2:]:
         cp.wait()
     wg_x.wait()
     wu_x.wait()
     wd_x.wait()
-    for cp in (a_all, b_all, c_all):
+    for cp in a_x + b_x + c_x:
         cp.wait_send()
     px = parts_out(Q, cap)
     gc = 8 * cap
@@ -465,13 +461,15 @@
     KW = token_keys.shape[1]
     D = residual.shape[1]
     half = D // 2
-    wide = half // 2
     topk = expert_ids.shape[1]
     FH = w_gate.shape[2]
     cap = max(2, -(-(T * topk) // E))
     Q = TILE // cap
     piece = HEAD_WIDTH
     C = half // (Q * piece)
+    A = C // 2
+    B = C - A
+    lanes = half // C // 2
     orow = out_weight.shape[0]
     hbm = pl.BlockSpec(memory_space=pltpu.HBM)
     V = pltpu.VMEM
@@ -486,9 +484,8 @@
         V((S * features // HEAD_WIDTH, HEAD_WIDTH), F32), V((8, KW), F32), V((8, KW), F32),
         V((E * TILE, HEAD_WIDTH), F32), V((E * TILE, HEAD_WIDTH), BF16),
         V((N * TILE, HEAD_WIDTH), BF16), V((N * S, 2 * orow), BF16),
-        V((E * TILE, wide // 2), BF16), V((E * TILE, wide // 2), BF16),
-        V((E * TILE, wide // 2), BF16), V((I, O * TILE, wide // 2), BF16),
-        V((O * TILE, wide // 2), BF16), V((O * TILE, wide // 2), BF16),
+        V((C, E * TILE, lanes), BF16), V((A, E * TILE, lanes), BF16),
+        V((B, I, O * TILE, lanes), BF16), V((B, O * TILE, lanes), BF16), V((B, O * TILE, lanes), BF16),
         V((T, D), F32), V((T, half), F32), V((T, half), F32),
         V((Q * T, E * TILE), F32), V((Q * T, E * TILE), F32), V((Q * T, E * TILE), F32),
         V((C, E * TILE, piece), BF16), V((C, E * TILE, piece), BF16), V((E * cap, half), BF16),
@@ -496,7 +493,7 @@
         V((C, E * TILE, piece), BF16), V((C, E * TILE, piece), BF16),
         V((T, half), F32), V((T, half), F32),
         dma((8,)), dma((2,)), dma((5,)), dma((7 + C,)), dma((7 + C,)),
-        *[dma((1,))] * 8, *[dma((C,))] * 4,
+        *[dma((1,))] * 2, *[dma((A,))] * 2, *[dma((B,))] * 4, *[dma((C,))] * 4,
     ]
     return pl.pallas_call(
         functools.partial(kernel, E, I, cap),

time: 42.4 us -> 41 us (0.967)
  Pallas kernels: 41.7 us -> 40.2 us
    pallas_call x1, Pallas kernels: 41.7 us -> 40.2 us  [on_device(): pl.pallas_call(functools.partial(kernel, E, I, cap), out_shape=pltpu.VMEM...]
where the time goes in v3:
time: 41 us; the launch traced here: 40.8 us
  Pallas kernels  40.2 us (98%)
  local copies, waits for them, and re-layouts  0.62 us (2%)
    pallas_call x1, Pallas kernels, on_device(): pl.pallas_call(functools.partial(kernel, E, I, cap), out_shape=pltpu.VMEM...  40.2 us

profile of v3, /device:TPU:0, one launch (start us, length us, event | category | flops | bytes accessed | tf_op | source)
XLA Modules:
  0.0 40.8 jit_solution(11808247166239755735)
XLA Ops:
  0.0 40.2 %shard_map.136 = bf16[4,4096]{1,0:T(4,128)(2,1)S(1)} custom-call(bf16[4,8192]{1,0:T(4,128)(2,1)} %q_hbm.1, bf16[4,512]{1,0:T(4,128)(2,1)} %tk_hbm.1, bf16[4,512]{1,0:T(4,128)(2,1)} %tv_hbm.1, s32[4]{0:T(128)} %kv_hbm.1, bf16[4,4096]{1,0:T(4,128)(2,1)} %res_hbm.1, bf16[4096]{0:T(1024)(128)(2,1)} %gain_hbm.1, s32[8,8]{1,0:T(8,128)} %ids_hbm.1, f32[8,8]{1,0:T(8,128)} %rw_hbm.1, ...), custom_call_target="tpu_custom_call" | custom-call | tf_op jit(solution)/shard_map/pallas_call | solution.py:498
  40.2 0.6 %copy.16 = bf16[4,4096]{1,0:T(4,128)(2,1)} copy(bf16[4,4096]{1,0:T(4,128)(2,1)S(1)} %shard_map.136) | data formatting | bytes 65536

commit v4 on v3

--- a/solution.py
+++ b/solution.py
@@ -10,6 +10,8 @@
 
 HEAD_WIDTH = 128
 TILE = 16
+CHUNKS = 4
+RETURNS = 2
 MESH = pl.DeviceIdType.MESH
 F32 = jnp.float32
 BF16 = jnp.bfloat16
@@ -28,30 +30,12 @@
     )
 
 
-def parts_out(Q, cap):
-    return permutation(
-        8 * Q * cap,
-        lambda a: ((a // cap) % 8) * TILE + (a // (8 * cap)) * cap + a % cap,
-    )
-
-
-def parts_in(Q, cap):
-    return permutation(
-        8 * Q * cap,
-        lambda a: ((a % TILE) // cap) * 8 * cap + (a // TILE) * cap + a % cap,
-    )
-
-
-def send_order(C):
-    return list(range(C // 2, C)) + list(range(C // 2))
-
-
 def dot(a, b):
     return jnp.dot(a, b, preferred_element_type=F32)
 
 
 def kernel(
-    E, I, cap,
+    E, I, cap, C, direct, Z,
     q_hbm, tk_hbm, tv_hbm, kv_hbm, res_hbm, gain_hbm, ids_hbm, rw_hbm,
     k_hbm, v_hbm, ow_hbm, wg_hbm, wu_hbm, wd_hbm,
     out_ref,
@@ -79,10 +63,7 @@
     D = res_ref.shape[1]
     half = D // 2
     hpc = heads // E
-    Q = TILE // cap
-    piece = HEAD_WIDTH
-    step = Q * piece
-    C = half // step
+    step = half // C
     FH = wg_hbm.shape[2]
     orow = ow_hbm.shape[0]
     drow = wd_hbm.shape[1]
@@ -236,15 +217,14 @@
     res_x = beside(resb.at[:, other], resp, 1)
     res_x.start()
 
-    lanes_all = E * TILE
+    lanes_all = E * cap
     lane = lax.broadcasted_iota(jnp.int32, (T, lanes_all), 1)
     tok = lax.broadcasted_iota(jnp.int32, (T, lanes_all), 0)
-    lm = lane // TILE
+    lm = lane // cap
     le = jnp.zeros((T, lanes_all), jnp.int32)
     for k in range(bits):
         flip = (lm // (1 << k)) % 2
         le = le + jnp.where(flip == 1, place[k][1], place[k][0])
-    lq = (lane // cap) % Q
     ls = lane % cap
     ids = ids_ref[...]
     rw = rw_ref[...]
@@ -262,11 +242,9 @@
     weight = weight * chosen
     high = weight.astype(BF16).astype(F32)
     low = weight - high
-    for p in range(Q):
-        here = lq == p
-        tts[p * T:(p + 1) * T, :] = jnp.where(here, chosen, 0.0)
-        whi[p * T:(p + 1) * T, :] = jnp.where(here, high, 0.0)
-        wlo[p * T:(p + 1) * T, :] = jnp.where(here, low, 0.0)
+    tts[...] = chosen
+    whi[...] = high
+    wlo[...] = low
 
     wcopies[1].wait()
     ow_x.wait()
@@ -280,10 +258,9 @@
                 blk[h * 8 * S:(h + 1) * 8 * S]
             )
     lanes = step // 2
-    direct = C // 2
     inner = range(I - 1, 0, -1)
     outer = range(O - 1, 0, -1)
-    for k in send_order(C):
+    for k in [*range(direct, C), *range(direct)]:
         y = [
             dot(asm[...], ow[:, k * step + j * lanes:k * step + (j + 1) * lanes]) for j in (0, 1)
         ]
@@ -293,17 +270,17 @@
             for m in far_first:
                 to_peer(
                     ys.at[k, rows_at(order[m], 1)], rsa.at[k, rows_at(order[m], 1)],
-                    sa.at[k], ra.at[k], m,
+                    sa.at[0], ra.at[k], m,
                 ).start()
         else:
             b = k - direct
             for p in inner:
                 to_peer(
-                    ys.at[k, rows_at(p * O, O)], rsb.at[b, p], sb.at[b], rb.at[b], p
+                    ys.at[k, rows_at(p * O, O)], rsb.at[b, p], sb.at[0], rb.at[b], p
                 ).start()
-    a_x = [whole(rsa.at[k, rows_at(1, E - 1)], sa.at[k], ra.at[k]) for k in range(direct)]
-    b_x = [whole(rsb.at[b, pl.ds(1, I - 1)], sb.at[b], rb.at[b]) for b in range(C - direct)]
-    c_x = [whole(rsc.at[b, rows_at(1, O - 1)], sc.at[b], rc.at[b]) for b in range(C - direct)]
+    a_x = [whole(rsa.at[k, rows_at(1, E - 1)], sa.at[0], ra.at[k]) for k in range(direct)]
+    b_x = [whole(rsb.at[b, pl.ds(1, I - 1)], sb.at[0], rb.at[b]) for b in range(C - direct)]
+    c_x = [whole(rsc.at[b, rows_at(1, O - 1)], sc.at[0], rc.at[b]) for b in range(C - direct)]
     kept = []
     for b in range(C - direct):
         b_x[b].wait_recv()
@@ -314,7 +291,7 @@
         kept.append(relay[0:TILE])
         for o in outer:
             to_peer(
-                zb.at[b, rows_at(o, 1)], rsc.at[b, rows_at(o, 1)], sc.at[b], rc.at[b], o * I
+                zb.at[b, rows_at(o, 1)], rsc.at[b, rows_at(o, 1)], sc.at[0], rc.at[b], o * I
             ).start()
 
     res_x.wait()
@@ -329,19 +306,15 @@
         cols = slice(k * step, (k + 1) * step)
         hidden = base[:, cols] + jnp.concatenate([total[:T], total[T:]], axis=1)
         hs[:, cols] = hidden
-        stacked = jnp.concatenate(
-            [hidden[:, p * piece:(p + 1) * piece] for p in range(Q)], axis=0
-        ).astype(BF16)
         picked = lax.dot_general(
-            table, stacked, (((0,), (0,)), ((), ())), preferred_element_type=F32
-        ).astype(BF16)
-        xb[k] = picked
+            table, hidden.astype(BF16), (((0,), (0,)), ((), ())), preferred_element_type=F32
+        )
+        for m in range(E):
+            xb[k, m] = picked[m * cap:(m + 1) * cap].astype(BF16)
         for m in far_first:
-            to_peer(
-                xb.at[k, rows_at(m, 1)], xr.at[k, rows_at(m, 1)], sx.at[k], rx.at[k], m
-            ).start()
-        xr[k, 0:TILE] = picked[0:TILE]
-        x_x.append(whole(xr.at[k, rows_at(1, E - 1)], sx.at[k], rx.at[k]))
+            to_peer(xb.at[k, m], xr.at[k, m], sx.at[0], rx.at[k], m).start()
+        xr[k, 0] = picked[0:cap].astype(BF16)
+        x_x.append(whole(xr.at[k, pl.ds(1, E - 1)], sx.at[0], rx.at[k]))
 
     for k in range(direct):
         a_x[k].wait_recv()
@@ -361,10 +334,9 @@
     wg_x.wait()
     wu_x.wait()
     wd_x.wait()
-    for cp in a_x + b_x + c_x:
-        cp.wait_send()
-    px = parts_out(Q, cap)
-    gc = 8 * cap
+    whole(rsa.at[:, rows_at(1, E - 1)], sa.at[0], ra.at[0]).wait_send()
+    whole(rsb.at[:, pl.ds(1, I - 1)], sb.at[0], rb.at[0]).wait_send()
+    whole(rsc.at[:, rows_at(1, O - 1)], sc.at[0], rc.at[0]).wait_send()
     rows = E * cap
     gain = gain_ref[mine].astype(F32).reshape(1, half)
     square = jnp.zeros((rows, 1), F32)
@@ -372,15 +344,10 @@
     gates, ups = slice(128, 128 + F), slice(128 + F, 128 + 2 * F)
     for k in range(C):
         x_x[k].wait_recv()
-        blk = [
-            dot(px, xr[k, grp * 8 * TILE:(grp + 1) * 8 * TILE, :]) for grp in range(E // 8)
-        ]
-        for p in range(Q):
-            part = jnp.concatenate([v[p * gc:(p + 1) * gc] for v in blk], axis=0)
-            square = square + jnp.sum(part * part, axis=1, keepdims=True)
-            cols = slice(k * step + p * piece, k * step + (p + 1) * piece)
-            xs[:, cols] = (part * gain[:, cols]).astype(BF16)
         feats = slice(k * step, (k + 1) * step)
+        part = xr[k].astype(F32).reshape(rows, step)
+        square = square + jnp.sum(part * part, axis=1, keepdims=True)
+        xs[:, feats] = (part * gain[:, feats]).astype(BF16)
         if k == 0:
             gus[:, gates] = dot(xs[:, feats], wg[feats, :])
         else:
@@ -405,44 +372,32 @@
     up = (gus[:, 128 + F:128 + 2 * F] + gur[:, 128 + F:128 + 2 * F]) * scale
     hid[...] = (gate * up).astype(BF16)
 
-    pb = parts_in(Q, cap)
+    stepz = half // Z
     z_x = []
-    for k in range(C):
-        o = dot(hid[...], wd[:, k * step:(k + 1) * step]).astype(BF16)
-        for grp in range(E // 8):
-            blk = jnp.concatenate([
-                o[grp * gc:(grp + 1) * gc, p * piece:(p + 1) * piece] for p in range(Q)
-            ], axis=0)
-            zs[k, grp * 8 * TILE:(grp + 1) * 8 * TILE, :] = dot(pb, blk).astype(BF16)
+    for k in range(Z):
+        o = dot(hid[...], wd[:, k * stepz:(k + 1) * stepz])
+        for m in range(E):
+            zs[k, m] = o[m * cap:(m + 1) * cap].astype(BF16)
         for m in far_first:
-            to_peer(
-                zs.at[k, rows_at(m, 1)], zr.at[k, rows_at(m, 1)], sz.at[k], rz.at[k], m
-            ).start()
-        zr[k, 0:TILE] = zs[k, 0:TILE]
-        z_x.append(whole(zr.at[k, rows_at(1, E - 1)], sz.at[k], rz.at[k]))
-
-    for cp in x_x:
-        cp.wait_send()
+            to_peer(zs.at[k, m], zr.at[k, m], sz.at[0], rz.at[k], m).start()
+        zr[k, 0] = o[0:cap].astype(BF16)
+        z_x.append(whole(zr.at[k, pl.ds(1, E - 1)], sz.at[0], rz.at[k]))
+
+    whole(xr.at[:, pl.ds(1, E - 1)], sx.at[0], rx.at[0]).wait_send()
     wh = whi[...].astype(BF16)
     wl = wlo[...].astype(BF16)
     own = c == 0
-    f_x = []
-    for k in range(C):
+    for k in range(Z):
         z_x[k].wait_recv()
-        part = dot(wh, zr[k]) + dot(wl, zr[k])
-        cols = slice(k * step, (k + 1) * step)
-        updated = hs[:, cols] + jnp.concatenate(
-            [part[p * T:(p + 1) * T] for p in range(Q)], axis=1
-        )
+        part = zr[k].astype(F32).reshape(rows, stepz).astype(BF16)
+        cols = slice(k * stepz, (k + 1) * stepz)
+        updated = hs[:, cols] + dot(wh, part) + dot(wl, part)
         ub[:, cols] = updated
-        f_x.append(beside(ub.at[:, pl.ds(k * step, step)], up_.at[:, pl.ds(k * step, step)], 7 + k))
-        f_x[k].start()
-        at = pl.ds(pl.multiple_of(c * half + k * step, step), step)
+        beside(ub.at[:, pl.ds(k * stepz, stepz)], up_.at[:, pl.ds(k * stepz, stepz)], 7).start()
+        at = pl.ds(pl.multiple_of(c * half + k * stepz, stepz), stepz)
         out_ref[:, at] = jnp.where(own, updated[:S], updated[S:]).astype(BF16)
-    for cp in z_x:
-        cp.wait_send()
-    for cp in f_x:
-        cp.wait()
+    whole(zr.at[:, pl.ds(1, E - 1)], sz.at[0], rz.at[0]).wait_send()
+    beside(ub, up_, 7).wait()
     got = up_[...]
     out_ref[:, other] = jnp.where(own, got[:S], got[S:]).astype(BF16)
 
@@ -464,12 +419,12 @@
     topk = expert_ids.shape[1]
     FH = w_gate.shape[2]
     cap = max(2, -(-(T * topk) // E))
-    Q = TILE // cap
-    piece = HEAD_WIDTH
-    C = half // (Q * piece)
+    C = CHUNKS
+    Z = RETURNS
     A = C // 2
     B = C - A
-    lanes = half // C // 2
+    step = half // C
+    lanes = step // 2
     orow = out_weight.shape[0]
     hbm = pl.BlockSpec(memory_space=pltpu.HBM)
     V = pltpu.VMEM
@@ -487,16 +442,17 @@
         V((C, E * TILE, lanes), BF16), V((A, E * TILE, lanes), BF16),
         V((B, I, O * TILE, lanes), BF16), V((B, O * TILE, lanes), BF16), V((B, O * TILE, lanes), BF16),
         V((T, D), F32), V((T, half), F32), V((T, half), F32),
-        V((Q * T, E * TILE), F32), V((Q * T, E * TILE), F32), V((Q * T, E * TILE), F32),
-        V((C, E * TILE, piece), BF16), V((C, E * TILE, piece), BF16), V((E * cap, half), BF16),
+        V((T, E * cap), F32), V((T, E * cap), F32), V((T, E * cap), F32),
+        V((C, E, cap, step), BF16), V((C, E, cap, step), BF16), V((E * cap, half), BF16),
         V((E * cap, wout), F32), V((E * cap, wout), F32), V((E * cap, 2 * FH), BF16),
-        V((C, E * TILE, piece), BF16), V((C, E * TILE, piece), BF16),
+        V((Z, E, cap, half // Z), BF16), V((Z, E, cap, half // Z), BF16),
         V((T, half), F32), V((T, half), F32),
-        dma((8,)), dma((2,)), dma((5,)), dma((7 + C,)), dma((7 + C,)),
-        *[dma((1,))] * 2, *[dma((A,))] * 2, *[dma((B,))] * 4, *[dma((C,))] * 4,
+        dma((8,)), dma((2,)), dma((5,)), dma((8,)), dma((8,)),
+        dma((1,)), dma((1,)), dma((1,)), dma((A,)), dma((1,)), dma((B,)), dma((1,)), dma((B,)),
+        dma((1,)), dma((C,)), dma((1,)), dma((Z,)),
     ]
     return pl.pallas_call(
-        functools.partial(kernel, E, I, cap),
+        functools.partial(kernel, E, I, cap, C, A, Z),
         out_shape=pltpu.VMEM((S, D), BF16),
         in_specs=[hbm] * 14,
         out_specs=pl.BlockSpec(memory_space=pltpu.VMEM),

time: 41 us -> 40.6 us (level)
  no operation moved by 1% of the time
where the time goes in v4:
time: 40.6 us; the launch traced here: 40.4 us
  Pallas kernels  39.8 us (98%)
  local copies, waits for them, and re-layouts  0.62 us (2%)
    pallas_call x1, Pallas kernels, on_device(): pl.pallas_call(functools.partial(kernel, E, I, cap, C, A, Z), out_shape=p...  39.8 us

profile of v4, /device:TPU:0, one launch (start us, length us, event | category | flops | bytes accessed | tf_op | source)
XLA Modules:
  0.0 40.4 jit_solution(6262393093510512401)
XLA Ops:
  0.0 39.8 %shard_map.136 = bf16[4,4096]{1,0:T(4,128)(2,1)S(1)} custom-call(bf16[4,8192]{1,0:T(4,128)(2,1)} %q_hbm.1, bf16[4,512]{1,0:T(4,128)(2,1)} %tk_hbm.1, bf16[4,512]{1,0:T(4,128)(2,1)} %tv_hbm.1, s32[4]{0:T(128)} %kv_hbm.1, bf16[4,4096]{1,0:T(4,128)(2,1)} %res_hbm.1, bf16[4096]{0:T(1024)(128)(2,1)} %gain_hbm.1, s32[8,8]{1,0:T(8,128)} %ids_hbm.1, f32[8,8]{1,0:T(8,128)} %rw_hbm.1, ...), custom_call_target="tpu_custom_call" | custom-call | tf_op jit(solution)/shard_map/pallas_call | solution.py:454
  39.8 0.6 %copy.16 = bf16[4,4096]{1,0:T(4,128)(2,1)} copy(bf16[4,4096]{1,0:T(4,128)(2,1)S(1)} %shard_map.136) | data formatting | bytes 65536

commit v5 on v4

--- a/solution.py
+++ b/solution.py
@@ -178,7 +178,7 @@
         return pltpu.make_async_remote_copy(
             src_ref=att.at[rows_at(peer[m], 1)], dst_ref=ratt.at[rows_at(2 * order[m] + c, 1)],
             send_sem=s1.at[0], recv_sem=r1.at[0],
-            device_id={"expert": peer[m], "replica": side[k]}, device_id_type=MESH,
+            device_id={"expert": peer[m], "replica": k if m else side[k]}, device_id_type=MESH,
         )
 
     def to_peer(src, dst, send, recv, m):

time: 40.6 us -> 40.6 us (level)
  no operation moved by 1% of the time
where the time goes in v5:
time: 40.6 us; the launch traced here: 40.4 us
  Pallas kernels  39.8 us (98%)
  local copies, waits for them, and re-layouts  0.62 us (2%)
    pallas_call x1, Pallas kernels, on_device(): pl.pallas_call(functools.partial(kernel, E, I, cap, C, A, Z), out_shape=p...  39.8 us

profile of v5, /device:TPU:0, one launch (start us, length us, event | category | flops | bytes accessed | tf_op | source)
XLA Modules:
  0.0 40.4 jit_solution(15101846101893901704)
XLA Ops:
  0.0 39.8 %shard_map.136 = bf16[4,4096]{1,0:T(4,128)(2,1)S(1)} custom-call(bf16[4,8192]{1,0:T(4,128)(2,1)} %q_hbm.1, bf16[4,512]{1,0:T(4,128)(2,1)} %tk_hbm.1, bf16[4,512]{1,0:T(4,128)(2,1)} %tv_hbm.1, s32[4]{0:T(128)} %kv_hbm.1, bf16[4,4096]{1,0:T(4,128)(2,1)} %res_hbm.1, bf16[4096]{0:T(1024)(128)(2,1)} %gain_hbm.1, s32[8,8]{1,0:T(8,128)} %ids_hbm.1, f32[8,8]{1,0:T(8,128)} %rw_hbm.1, ...), custom_call_target="tpu_custom_call" | custom-call | tf_op jit(solution)/shard_map/pallas_call | solution.py:454
  39.8 0.6 %copy.16 = bf16[4,4096]{1,0:T(4,128)(2,1)} copy(bf16[4,4096]{1,0:T(4,128)(2,1)S(1)} %shard_map.136) | data formatting | bytes 65536
